TPU v7x, 32 devices: a whole 2x2x4 slice. The times are simulated.
32 devices in a mesh: sub: 8 (over z, x), fdr: 4 (over y, core).
Axes of the slice: x: 2, y: 2, z: 4, core: 2. Of those that a mesh axis runs over, the one named last changes fastest.
Arguments:
- inverse: bfloat16 [1024, 256, 256], P(('sub', 'fdr')), may hold values from -1 to 1
- cost: float32 [1024, 256, 128], P(('sub', 'fdr')), may hold values from -6 to 6
- lower_limit: float32 [1024, 256], P(('sub', 'fdr')), may hold values from -1.5 to -0.5
- upper_limit: float32 [1024, 256], P(('sub', 'fdr')), may hold values from 0.5 to 1.5
- iface_rows: int32 [1024, 6], P(('sub', 'fdr')), may hold values from 0 to 255, as said below
- substation_of: int32 [1024], P(('sub', 'fdr')), may hold values from 0 to 255, as said below
- live_count: int32 [32], P(('sub', 'fdr')), may hold values from 16 to 32
- reserve_weight: float32 [256], P('sub'), may hold values from 0.5 to 4
- reserve_target: float32 [256, 6, 128], P('sub'), may hold values from -6 to 6
Outputs:
- duals: float32 [1024, 6, 128], P(('sub', 'fdr'))
- consensus: float32 [256, 6, 128], P('sub')
- residual_norms: float32 [5, 2], replicated
- setpoints: float32 [1024, 256, 128], P(('sub', 'fdr'))
Inputs may be any that keep to these rules, and one draw needn't show every extreme that they name: `iface_rows`: each feeder's 6 interface rows are distinct. `substation_of`: of one device's 32 slots at most 6 hang from substations of one owner block (substations k * 32 to k * 32 + 31); for each index of fdr some block gets exactly 6 slots from every device with that index. `live_count`: a device's live feeders fill its first slots; the other slots hold unused data.
All inputs are finite; a program needn't handle non-finite values.
Results may differ from a plain program's by a relative error of at most 0.0069.
Values sent between devices are 32-bit elements; how exact they have to be, the bound alone decides.
No kernel may reach another device: no remote copies, remote signals or barrier semaphores. Data moves between devices by JAX's collectives and lax.ppermute only.
A program may use at most 128 MiB of HBM per device.

v0:
```python
import jax
import jax.numpy as jnp
from jax import lax
from jax.sharding import PartitionSpec as P

ITERS = 5


penalty = 2.0


def shards(
    inverse,
    cost,
    lower_limit,
    upper_limit,
    iface_rows,
    substation_of,
    live_count,
    reserve_weight,
    reserve_target,
):
    slot_count = inverse.shape[0]
    iface_count = iface_rows.shape[1]
    scenarios = cost.shape[2]
    flat_width = iface_count * scenarios
    sub_count = lax.axis_size("sub")
    owned_count = reserve_weight.shape[0]
    total_sub = owned_count * sub_count
    sub_index = lax.axis_index("sub")
    fdr_index = lax.axis_index("fdr")
    active = (jnp.arange(slot_count, dtype=jnp.int32) < live_count[0]).astype(jnp.float32)
    membership = (substation_of[:, None] == jnp.arange(total_sub, dtype=jnp.int32)[None, :]).astype(
        jnp.float32
    ) * active[:, None]
    tallied = lax.psum(jnp.sum(membership, axis=0), ("sub", "fdr"))
    flat_target = reserve_target.reshape(owned_count, flat_width)
    first_row = sub_index * owned_count
    dual_mask = (fdr_index == 0).astype(jnp.float32)
    overflow = max(1, slot_count // (2 * sub_count))
    capacity = max(2, slot_count // sub_count + overflow)
    slot_total = sub_count * capacity
    group_of = substation_of // owned_count
    group_hot = (group_of[:, None] == jnp.arange(sub_count, dtype=jnp.int32)[None, :]).astype(
        jnp.int32
    )
    earlier = jnp.cumsum(group_hot, axis=0) - group_hot
    slot_rank = jnp.sum(earlier * group_hot, axis=1)
    position = group_of * capacity + slot_rank
    slot_match = position[:, None] == jnp.arange(slot_total, dtype=jnp.int32)[None, :]
    slot_hot = slot_match.astype(jnp.float32)
    slot_ids = jnp.sum(slot_match.astype(jnp.int32) * (substation_of + 1)[:, None], axis=0) - 1
    arrived_ids = lax.all_to_all(slot_ids, "sub", split_axis=0, concat_axis=0, tiled=True)
    arrived_hot = (
        (arrived_ids - sub_index * owned_count)[:, None]
        == jnp.arange(owned_count, dtype=jnp.int32)[None, :]
    ).astype(jnp.float32)
    own_members = lax.dynamic_slice_in_dim(tallied, first_row, owned_count, 0)
    feeder_index = jnp.arange(slot_count, dtype=jnp.int32)[:, None]
    scaled_dual = jnp.zeros((slot_count, iface_count, scenarios), jnp.float32)
    local_consensus = jnp.zeros((slot_count, iface_count, scenarios), jnp.float32)
    anchor = jnp.zeros((slot_count, inverse.shape[1], scenarios), jnp.float32)
    old_rows = jnp.zeros((owned_count, flat_width), jnp.float32)
    sums_list = []
    for iteration in range(ITERS):
        right_side = (
            (anchor - cost)
            .at[feeder_index, iface_rows]
            .add(penalty * (local_consensus - scaled_dual))
            .astype(jnp.bfloat16)
        )
        primal = jnp.einsum("fkj,fjs->fks", inverse, right_side, preferred_element_type=jnp.float32)
        anchor = jnp.clip(primal, lower_limit[:, :, None], upper_limit[:, :, None])
        boundary = jnp.take_along_axis(primal, iface_rows[:, :, None], axis=1)
        outgoing = ((boundary + scaled_dual) * active[:, None, None]).reshape(
            slot_count, flat_width
        )
        packed = jnp.einsum("fn,fc->nc", slot_hot, outgoing, precision=lax.Precision.HIGHEST)
        arrived = lax.all_to_all(packed, "sub", split_axis=0, concat_axis=0, tiled=True)
        block_sums = jnp.einsum("no,nc->oc", arrived_hot, arrived, precision=lax.Precision.HIGHEST)
        collected = lax.psum(block_sums, "fdr")
        new_rows = (collected + reserve_weight[:, None] * flat_target) / (
            own_members + reserve_weight
        )[:, None]
        dual_local = dual_mask * jnp.sum(own_members[:, None] * (new_rows - old_rows) ** 2)
        old_rows = new_rows
        reply = jnp.einsum("no,oc->nc", arrived_hot, new_rows, precision=lax.Precision.HIGHEST)
        returned = lax.all_to_all(reply, "sub", split_axis=0, concat_axis=0, tiled=True)
        local_consensus = jnp.einsum(
            "fn,nc->fc", slot_hot, returned, precision=lax.Precision.HIGHEST
        ).reshape(slot_count, iface_count, scenarios)
        mismatch = boundary - local_consensus
        scaled_dual = (scaled_dual + mismatch) * active[:, None, None]
        primal_local = jnp.sum(active[:, None, None] * mismatch**2)
        primal_sum, dual_sum = lax.psum((primal_local, dual_local), ("sub", "fdr"))
        sums_list.append(jnp.stack([primal_sum, dual_sum]))
    stacked = jnp.stack(sums_list)
    residual_norms = jnp.sqrt(stacked) * jnp.array([1.0, penalty], jnp.float32)[None, :]
    consensus = old_rows.reshape(owned_count, iface_count, scenarios)
    return (penalty * scaled_dual, consensus, residual_norms, anchor * active[:, None, None])


def solution(mesh):
    placed = (
        P(("sub", "fdr"), None, None),
        P(("sub", "fdr"), None, None),
        P(("sub", "fdr"), None),
        P(("sub", "fdr"), None),
        P(("sub", "fdr"), None),
        P(("sub", "fdr")),
        P(("sub", "fdr")),
        P("sub"),
        P("sub", None, None),
    )
    return jax.shard_map(
        shards,
        mesh=mesh,
        in_specs=placed,
        out_specs=(
            P(("sub", "fdr"), None, None),
            P("sub", None, None),
            P(),
            P(("sub", "fdr"), None, None),
        ),
        check_vma=False,
    )
```

profile of v0, /device:TPU:0, one launch (start us, length us, event | category | flops | bytes accessed | tf_op | source)
XLA Modules:
  0.0 612.7 jit_solution(17046164565639930385)
XLA Ops:
  9.0 7.3 %all-to-all-start = ((s32[8,6,1]{1,2,0:T(1,128)}), s32[8,6,1]{1,2,0:T(1,128)S(1)}, u32[]{:S(2)}, u32[]{:S(2)}) async-start(s32[8,6,1]{1,2,0:T(1,128)} %bitcast.5), calls=%async_computation | async-start | bytes 8192 | tf_op jit(solution)/shard_map/all_to_all | solution.py:53
  17.7 5.6 copy.151
  23.3 4.6 broadcast_subtract_fusion
  29.0 20.1 %scatter_fusion = f32[32,256,128]{2,1,0:T(8,128)} fusion(f32[32,256,128]{2,1,0:T(8,128)} %broadcast_subtract_fusion, s32[192]{0:T(256)S(1)} %reshape.165, f32[192,128]{1,0:T(8,128)S(1)} %broadcast.263), kind=kCustom, calls=%fused_computation.5 | custom fusion | flops 24576 | bytes 296448 | tf_op jit(solution)/shard_map/scatter-add | solution.py:69
  49.1 9.3 %minimum_subtract_fusion.3 = (f32[32,256,128]{1,2,0:T(8,128)}, f32[32,256,128]{1,2,0:T(8,128)}) fusion(f32[32,256,128]{1,2,0:T(8,128)} %copy.151, f32[32,256]{1,0:T(8,128)S(1)} %copy-done.1, f32[32,256]{1,0:T(8,128)S(1)} %copy-done.2, bf16[32,256,256]{2,1,0:T(8,128)(2,1)} %param.12, f32[32,256,128]{2,1,0:T(8,128)} %scatter_fusion), kind=kOutput, calls=%fused_computation.14 | convolution fusion | flops 541065216 | bytes 21037056 | tf_op jit(solution)/shard_map/fkj,fjs->fks/dot_general | solution.py:72
  58.5 5.6 copy.144
  64.0 4.6 gather_fusion
  69.7 5.9 all-to-all-start.1
  75.8 40.8 %psum.113 = f32[256]{0:T(256)S(1)} all-reduce(f32[256]{0:T(256)S(1)} %select_reduce_fusion), channel_id=1, replica_groups=mesh['sub'=8,'fdr'=4] {'sub','fdr'}, use_global_device_ids=true, to_apply=%region_6.8 | all-reduce | flops 256 | bytes 2048 | tf_op jit(solution)/shard_map/psum | solution.py:36
  117.8 31.6 %all-reduce.7.cloned.1.call-done = f32[32,768]{1,0:T(8,128)} async-done(((f32[32,768]{1,0:T(8,128)}), f32[32,768]{1,0:T(8,128)}) %all-reduce.7.cloned.1.call-update) | async-done | bytes 98320 | tf_op jit(solution)/shard_map/psum | solution.py:81
  151.3 5.5 all-to-all-start.2
  156.9 5.6 copy.153
  162.5 2.2 all-to-all-done.2
  165.0 20.1 %scatter_fusion.1 = f32[32,256,128]{2,1,0:T(8,128)} fusion(f32[32,256,128]{2,1,0:T(8,128)} %copy.153, s32[192]{0:T(256)S(1)} %reshape.165, f32[192,128]{1,0:T(8,128)S(1)} %reshape.173), kind=kCustom, calls=%fused_computation.6 | custom fusion | flops 24576 | bytes 296448 | tf_op jit(solution)/shard_map/scatter-add | solution.py:69
  185.1 9.4 %minimum_subtract_fusion.2 = (f32[32,256,128]{1,2,0:T(8,128)}, f32[32,256,128]{1,2,0:T(8,128)}) fusion(f32[32,256,128]{1,2,0:T(8,128)} %copy.151, f32[32,256]{1,0:T(8,128)S(1)} %copy-done.1, f32[32,256]{1,0:T(8,128)S(1)} %copy-done.2, bf16[32,256,256]{2,1,0:T(8,128)(2,1)} %param.12, f32[32,256,128]{2,1,0:T(8,128)} %scatter_fusion.1), kind=kOutput, calls=%fused_computation.13 | convolution fusion | flops 541065216 | bytes 21037056 | tf_op jit(solution)/shard_map/fkj,fjs->fks/dot_general | solution.py:72
  194.4 5.6 copy.156
  200.0 4.6 gather_fusion.1
  205.0 11.3 %all_to_all.111 = f32[8,6,768]{2,1,0:T(8,128)S(1)} all-to-all(f32[8,6,768]{2,1,0:T(8,128)S(1)} %fusion.40), channel_id=1, replica_groups=mesh['sub'=8,'fdr'=4] {'sub'}, dimensions={0} | all-to-all | bytes 294912 | tf_op jit(solution)/shard_map/all_to_all | solution.py:79
  217.3 28.9 %all-reduce.9.cloned.1.call-done = f32[32,768]{1,0:T(8,128)} async-done(((f32[32,768]{1,0:T(8,128)}), f32[32,768]{1,0:T(8,128)}) %all-reduce.9.cloned.1.call-update) | async-done | bytes 98320 | tf_op jit(solution)/shard_map/psum | solution.py:81
  248.2 5.5 all-to-all-start.4
  253.7 5.6 copy.163
  261.8 20.1 %scatter_fusion.2 = f32[32,256,128]{2,1,0:T(8,128)} fusion(f32[32,256,128]{2,1,0:T(8,128)} %copy.163, s32[192]{0:T(256)S(1)} %reshape.165, f32[192,128]{1,0:T(8,128)S(1)} %reshape.179), kind=kCustom, calls=%fused_computation.7 | custom fusion | flops 24576 | bytes 296448 | tf_op jit(solution)/shard_map/scatter-add | solution.py:69
  281.9 9.4 %minimum_subtract_fusion.1 = (f32[32,256,128]{1,2,0:T(8,128)}, f32[32,256,128]{1,2,0:T(8,128)}) fusion(f32[32,256,128]{1,2,0:T(8,128)} %copy.151, f32[32,256]{1,0:T(8,128)S(1)} %copy-done.1, f32[32,256]{1,0:T(8,128)S(1)} %copy-done.2, bf16[32,256,256]{2,1,0:T(8,128)(2,1)} %param.12, f32[32,256,128]{2,1,0:T(8,128)} %scatter_fusion.2), kind=kOutput, calls=%fused_computation.12 | convolution fusion | flops 541065216 | bytes 21037056 | tf_op jit(solution)/shard_map/fkj,fjs->fks/dot_general | solution.py:72
  291.3 5.6 copy.166
  296.9 4.6 gather_fusion.2
  301.9 11.3 %all_to_all.112 = f32[8,6,768]{2,1,0:T(8,128)S(1)} all-to-all(f32[8,6,768]{2,1,0:T(8,128)S(1)} %fusion.38), channel_id=1, replica_groups=mesh['sub'=8,'fdr'=4] {'sub'}, dimensions={0} | all-to-all | bytes 294912 | tf_op jit(solution)/shard_map/all_to_all | solution.py:79
  314.1 28.9 %all-reduce.11.cloned.1.call-done = f32[32,768]{1,0:T(8,128)} async-done(((f32[32,768]{1,0:T(8,128)}), f32[32,768]{1,0:T(8,128)}) %all-reduce.11.cloned.1.call-update) | async-done | bytes 98320 | tf_op jit(solution)/shard_map/psum | solution.py:81
  345.0 5.5 all-to-all-start.6
  350.6 5.6 copy.173
  358.7 20.1 %scatter_fusion.3 = f32[32,256,128]{2,1,0:T(8,128)} fusion(f32[32,256,128]{2,1,0:T(8,128)} %copy.173, s32[192]{0:T(256)S(1)} %reshape.165, f32[192,128]{1,0:T(8,128)S(1)} %reshape.185), kind=kCustom, calls=%fused_computation.8 | custom fusion | flops 24576 | bytes 296448 | tf_op jit(solution)/shard_map/scatter-add | solution.py:69
  378.8 9.5 %minimum_subtract_fusion = (f32[32,256,128]{1,2,0:T(8,128)}, f32[32,256,128]{1,2,0:T(8,128)}) fusion(f32[32,256,128]{1,2,0:T(8,128)} %copy.151, f32[32,256]{1,0:T(8,128)S(1)} %copy-done.1, f32[32,256]{1,0:T(8,128)S(1)} %copy-done.2, bf16[32,256,256]{2,1,0:T(8,128)(2,1)} %param.12, f32[32,256,128]{2,1,0:T(8,128)} %scatter_fusion.3), kind=kOutput, calls=%fused_computation.11 | convolution fusion | flops 541065216 | bytes 21037056 | tf_op jit(solution)/shard_map/fkj,fjs->fks/dot_general | solution.py:72
  388.3 5.6 copy.176
  393.9 4.6 gather_fusion.3
  398.9 11.3 %all_to_all.113 = f32[8,6,768]{2,1,0:T(8,128)S(1)} all-to-all(f32[8,6,768]{2,1,0:T(8,128)S(1)} %fusion.36), channel_id=1, replica_groups=mesh['sub'=8,'fdr'=4] {'sub'}, dimensions={0} | all-to-all | bytes 294912 | tf_op jit(solution)/shard_map/all_to_all | solution.py:79
  411.2 29.0 %all-reduce.13.cloned.1.call-done = f32[32,768]{1,0:T(8,128)} async-done(((f32[32,768]{1,0:T(8,128)}), f32[32,768]{1,0:T(8,128)}) %all-reduce.13.cloned.1.call-update) | async-done | bytes 98320 | tf_op jit(solution)/shard_map/psum | solution.py:81
  442.1 5.5 all-to-all-start.8
  447.9 5.6 copy.183
  455.8 20.1 %scatter_fusion.4 = f32[32,256,128]{2,1,0:T(8,128)} fusion(f32[32,256,128]{2,1,0:T(8,128)} %copy.183, s32[192]{0:T(256)S(1)} %reshape.165, f32[192,128]{1,0:T(8,128)S(1)} %reshape.191), kind=kCustom, calls=%fused_computation.9 | custom fusion | flops 24576 | bytes 296448 | tf_op jit(solution)/shard_map/scatter-add | solution.py:69
  475.8 8.4 %minimum_multiply_fusion = (f32[32,256,128]{1,2,0:T(8,128)}, f32[32,256,128]{1,2,0:T(8,128)}) fusion(f32[32]{0:T(128)S(1)} %compare_convert_fusion, f32[32,256]{1,0:T(8,128)S(1)} %copy-done.1, f32[32,256]{1,0:T(8,128)S(1)} %copy-done.2, bf16[32,256,256]{2,1,0:T(8,128)(2,1)} %param.12, f32[32,256,128]{2,1,0:T(8,128)} %scatter_fusion.4), kind=kOutput, calls=%fused_computation.10 | convolution fusion | flops 541065216 | bytes 16842880 | tf_op jit(solution)/shard_map/fkj,fjs->fks/dot_general | solution.py:72
  484.2 5.6 copy.186
  489.8 4.6 gather_fusion.4
  494.8 11.3 %all_to_all.114 = f32[8,6,768]{2,1,0:T(8,128)S(1)} all-to-all(f32[8,6,768]{2,1,0:T(8,128)S(1)} %fusion.34), channel_id=1, replica_groups=mesh['sub'=8,'fdr'=4] {'sub'}, dimensions={0} | all-to-all | bytes 294912 | tf_op jit(solution)/shard_map/all_to_all | solution.py:79
  507.1 28.9 %all-reduce.15.cloned.1.call-done = f32[32,768]{1,0:T(8,128)} async-done(((f32[32,768]{1,0:T(8,128)}), f32[32,768]{1,0:T(8,128)}) %all-reduce.15.cloned.1.call-update) | async-done | bytes 98320 | tf_op jit(solution)/shard_map/psum | solution.py:81
  538.7 5.5 all-to-all-start.10
  544.2 5.6 copy.197
  555.3 43.2 %all-reduce = (f32[1]{0:T(128)}, f32[1]{0:T(128)}, f32[1]{0:T(128)}, f32[1]{0:T(128)}, f32[1]{0:T(128)}, /*index=5*/f32[1]{0:T(128)}, f32[1]{0:T(128)}, f32[1]{0:T(128)}, f32[1]{0:T(128)}, f32[1]{0:T(128)}) all-reduce(f32[1]{0:T(128)} %bitcast.21, f32[1]{0:T(128)} %bitcast.20, ...), channel_id=1, replica_groups=mesh['sub'=8,'fdr'=4] {'sub','fdr'}, use_global_device_ids=true, to_apply=%region_18.20 | all-reduce | flops 10 | bytes 80 | tf_op jit(solution)/shard_map/psum | solution.py:95
  598.4 2.6 maximum_bitcast_fusion
  602.7 2.5 maximum_bitcast_fusion.2
  (127 shorter events, 35.0 us)
Async XLA Ops:
  7.2 142.2 %copy-start = (f32[32,6,128]{2,0,1:T(8,128)S(1)}, f32[32,6,128]{2,0,1:T(8,128)}, u32[]{:S(2)}) copy-start(f32[32,6,128]{2,0,1:T(8,128)} %param.20) | copy-start | bytes 294916
  9.0 60.8 %all-to-all-start = ((s32[8,6,1]{1,2,0:T(1,128)}), s32[8,6,1]{1,2,0:T(1,128)S(1)}, u32[]{:S(2)}, u32[]{:S(2)}) async-start(s32[8,6,1]{1,2,0:T(1,128)} %bitcast.5), calls=%async_computation | async-start | bytes 8192 | tf_op jit(solution)/shard_map/all_to_all | solution.py:53
  23.3 25.8 %copy-start.1 = (f32[32,256]{1,0:T(8,128)S(1)}, f32[32,256]{1,0:T(8,128)}, u32[]{:S(2)}) copy-start(f32[32,256]{1,0:T(8,128)} %param.14) | copy-start | bytes 98308
  23.3 25.8 %copy-start.2 = (f32[32,256]{1,0:T(8,128)S(1)}, f32[32,256]{1,0:T(8,128)}, u32[]{:S(2)}) copy-start(f32[32,256]{1,0:T(8,128)} %param.15) | copy-start | bytes 98308
  58.4 17.2 %copy-start.5 = (s32[32]{0:T(128)S(1)}, s32[32]{0:T(128)}, u32[]{:S(2)}) copy-start(s32[32]{0:T(128)} %param.17) | copy-start | bytes 388
  58.4 59.2 %copy-start.3 = (f32[32]{0:T(128)S(1)}, f32[32]{0:T(128)}, u32[]{:S(2)}) copy-start(f32[32]{0:T(128)} %param.19) | copy-start | bytes 388
  69.7 46.9 %all-to-all-start.1 = ((f32[8,6,768]{2,1,0:T(8,128)}), f32[8,6,768]{2,1,0:T(8,128)S(1)}, u32[]{:S(2)}, u32[]{:S(2)}) async-start(f32[8,6,768]{2,1,0:T(8,128)} %fusion.42), calls=%async_computation.1 | async-start | bytes 393216 | tf_op jit(solution)/shard_map/all_to_all | solution.py:79
  75.6 73.8 %all-reduce.7.cloned.1.call-start = ((), (), s32[]{:S(2)}) async-start(), calls=%async_computation.11 | async-start | bytes 196608 | tf_op jit(solution)/shard_map/psum | solution.py:81
  151.3 13.3 %all-to-all-start.2 = ((f32[8,6,768]{2,1,0:T(8,128)}), f32[8,6,768]{2,1,0:T(8,128)S(1)}, u32[]{:S(2)}, u32[]{:S(2)}) async-start(f32[8,6,768]{2,1,0:T(8,128)} %all_to_all.77), calls=%async_computation.2 | async-start | bytes 393216 | tf_op jit(solution)/shard_map/all_to_all | solution.py:88
  156.8 89.4 %all-reduce.9.cloned.1.call-start = ((), (), s32[]{:S(2)}) async-start(), calls=%async_computation.12 | async-start | bytes 196608 | tf_op jit(solution)/shard_map/psum | solution.py:81
  248.2 13.3 %all-to-all-start.4 = ((f32[8,6,768]{2,1,0:T(8,128)}), f32[8,6,768]{2,1,0:T(8,128)S(1)}, u32[]{:S(2)}, u32[]{:S(2)}) async-start(f32[8,6,768]{2,1,0:T(8,128)} %all_to_all.82), calls=%async_computation.4 | async-start | bytes 393216 | tf_op jit(solution)/shard_map/all_to_all | solution.py:88
  253.7 89.4 %all-reduce.11.cloned.1.call-start = ((), (), s32[]{:S(2)}) async-start(), calls=%async_computation.13 | async-start | bytes 196608 | tf_op jit(solution)/shard_map/psum | solution.py:81
  345.0 13.3 %all-to-all-start.6 = ((f32[8,6,768]{2,1,0:T(8,128)}), f32[8,6,768]{2,1,0:T(8,128)S(1)}, u32[]{:S(2)}, u32[]{:S(2)}) async-start(f32[8,6,768]{2,1,0:T(8,128)} %all_to_all.87), calls=%async_computation.6 | async-start | bytes 393216 | tf_op jit(solution)/shard_map/all_to_all | solution.py:88
  350.5 89.6 %all-reduce.13.cloned.1.call-start = ((), (), s32[]{:S(2)}) async-start(), calls=%async_computation.14 | async-start | bytes 196608 | tf_op jit(solution)/shard_map/psum | solution.py:81
  442.1 13.3 %all-to-all-start.8 = ((f32[8,6,768]{2,1,0:T(8,128)}), f32[8,6,768]{2,1,0:T(8,128)S(1)}, u32[]{:S(2)}, u32[]{:S(2)}) async-start(f32[8,6,768]{2,1,0:T(8,128)} %all_to_all.92), calls=%async_computation.8 | async-start | bytes 393216 | tf_op jit(solution)/shard_map/all_to_all | solution.py:88
  447.6 88.4 %all-reduce.15.cloned.1.call-start = ((), (), s32[]{:S(2)}) async-start(), calls=%async_computation.15 | async-start | bytes 196608 | tf_op jit(solution)/shard_map/psum | solution.py:81
  538.7 15.0 %all-to-all-start.10 = ((f32[8,6,768]{2,1,0:T(8,128)}), f32[8,6,768]{2,1,0:T(8,128)S(1)}, u32[]{:S(2)}, u32[]{:S(2)}) async-start(f32[8,6,768]{2,1,0:T(8,128)} %all_to_all.97), calls=%async_computation.10 | async-start | bytes 393216 | tf_op jit(solution)/shard_map/all_to_all | solution.py:88
  544.2 61.3 %copy-start.4 = (f32[2]{0:T(128)S(1)}, f32[2]{0:T(128)}, u32[]{:S(2)}) copy-start(f32[2]{0:T(128)} %constant.68.clone) | copy-start | bytes 28
Sparse Core Ops, SparseCore 0:
  117.8 31.5 all-reduce.6
  217.4 28.7 all-reduce.8
  314.3 28.7 all-reduce.10
  411.3 28.7 all-reduce.12
  507.2 28.7 all-reduce.14
where the time goes:
time: 617 us; the launch traced here: 613 us
  waiting for transfers between devices  156 us (25%)
  blocking collectives  129 us (21%)
  other arithmetic  121 us (20%)
  local copies, waits for them, and re-layouts  91.1 us (15%)
  matrix products  56.4 us (9%)
  starting transfers between devices  41.1 us (7%)
  between operations  18.1 us (3%)
    psum x5, waiting for transfers between devices, shards(): collected = lax.psum(block_sums, 'fdr')  147 us
    scatter-add x5, other arithmetic, shards(): right_side = (anchor - cost).at[feeder_index, iface_rows].add(penalty * (...  100 us
    dot_general x5, matrix products, shards(): jnp.einsum('fkj,fjs->fks', inverse, right_side, preferred_element_type=jn...  46 us
    all_to_all x4, blocking collectives, shards(): lax.all_to_all(packed, 'sub', split_axis=0, concat_axis=0, tiled=True)  45 us
    psum x1, blocking collectives, shards(): primal_sum, dual_sum = lax.psum((primal_local, dual_local), ('sub', 'fdr'))  43.2 us
    psum x1, blocking collectives, shards(): tallied = lax.psum(jnp.sum(membership, axis=0), ('sub', 'fdr'))  40.8 us
    dot_general x5, local copies, waits for them, and re-layouts, shards(): jnp.einsum('fkj,fjs->fks', inverse, right_side, preferred_element_type=jn...  27.9 us
    all_to_all x5, starting transfers between devices, shards(): lax.all_to_all(reply, 'sub', split_axis=0, concat_axis=0, tiled=True)  27.6 us
  transfers between devices with their start and end apart: 12, of which 9 were waited for; matrix products, arithmetic and copies ran while one was open for 13% of the time, Pallas kernels for 0%

commit v1 on v0

v1 whole, which is shorter than its diff:
```python
import functools

import jax
import jax.numpy as jnp
from jax import lax
from jax.experimental import pallas as pl
from jax.experimental.pallas import tpu as pltpu
from jax.sharding import PartitionSpec as P

ITERS = 5
PENALTY = 2.0
LANES = 128
THIN = 16

f32 = jnp.float32
bf16 = jnp.bfloat16
i32 = jnp.int32


class Geometry:
    def __init__(self, slots, rows, ifc, scen, owned, n_sub, n_fdr):
        self.F, self.K, self.Q, self.C, self.S = slots, rows, ifc, scen, owned
        self.NB, self.G = n_sub, n_fdr
        self.D = n_sub * n_fdr
        overflow = max(1, slots // (2 * n_sub))
        cap = max(2, slots // n_sub + overflow)
        self.L = scen // n_fdr
        self.RP = n_fdr // 2
        self.R2 = -(-cap // self.RP)
        self.PR = self.R2 * self.RP
        self.Q2 = ifc // 2
        self.X = self.Q2 * self.R2
        self.stage_rows = self.G * self.X * self.NB
        self.id_lane = self.Q2 * self.PR * self.Q

    def off(self, q):
        q2, qp = divmod(q, 2)
        return (qp * self.RP * self.X + q2 * self.R2) * self.NB


def iota(shape, dim):
    return lax.broadcasted_iota(i32, shape, dim)


def group_mask(shape, g, width):
    lane = iota(shape, 1)
    return (lane >= g * width) & (lane < (g + 1) * width)


def roll(x, shift):
    shift = shift % LANES
    return pltpu.roll(x, shift, 1) if shift else x


def pack(geo, stage, send, chunk, off):
    n = geo.X * geo.NB
    for j in range(geo.G):
        acc = None
        for g in range(geo.G):
            v = roll(stage[g * n : (g + 1) * n, :], (g - j) * geo.L)
            acc = v if acc is None else jnp.where(group_mask((n, LANES), g, geo.L), v, acc)
        for x in range(geo.X):
            send[pl.ds(j * chunk + off + x, geo.NB, stride=geo.G * chunk), :] = acc[
                x * geo.NB : (x + 1) * geo.NB
            ]


def unpack(geo, recv, stage, chunk, off):
    n = geo.X * geo.NB
    parts = [
        jnp.concatenate(
            [
                recv[pl.ds(j * chunk + off + x, geo.NB, stride=geo.G * chunk), :]
                for x in range(geo.X)
            ],
            axis=0,
        )
        for j in range(geo.G)
    ]
    for g in range(geo.G):
        acc = None
        for j in range(geo.G):
            v = roll(parts[j], (j - g) * geo.L)
            acc = v if acc is None else jnp.where(group_mask((n, LANES), j, geo.L), v, acc)
        stage[g * n : (g + 1) * n, :] = acc


def dot(a, b):
    return jnp.dot(a, b, preferred_element_type=f32)


def limits(geo, lim, f):
    low = jnp.take_along_axis(lim[...], jnp.full((geo.K, LANES), f, i32), axis=1)
    high = jnp.take_along_axis(lim[...], jnp.full((geo.K, LANES), f + geo.F, i32), axis=1)
    return low, high


def feeder_first(geo, iface, sub, live, inverse, cost, lower, upper,
                 target, thin, lim, base, send, stage1, stage2, meta, count, rank):
    F, K, Q, NB, X = geo.F, geo.K, geo.Q, geo.NB, geo.X
    chunk = 2 * X + 2
    for k in range(NB):
        count[k] = 0

    def place(f, carry):
        k = lax.div(sub[f], geo.S)
        r = count[k]
        count[k] = r + 1
        rank[f] = r
        base[f] = (lax.rem(r, geo.RP) * X + lax.div(r, geo.RP)) * NB + k
        return carry

    lax.fori_loop(0, F, place, 0)
    stacked = jnp.concatenate(
        [lower[...], upper[...], jnp.zeros((LANES - 2 * F, K), f32)], axis=0
    )
    lim[...] = stacked.T
    stage1[...] = jnp.zeros_like(stage1)
    stage2[...] = jnp.zeros_like(stage2)
    meta[...] = jnp.zeros_like(meta)

    def body(f, carry):
        row = iota((THIN, K), 0)
        chosen = jnp.full((THIN, K), -1, i32)
        for q in range(Q):
            chosen = jnp.where(row == q, iface[f, q], chosen)
        hot = (iota((THIN, K), 1) == chosen).astype(f32).astype(bf16)
        full = inverse[f]
        few = dot(hot, full).astype(bf16)
        thin[f] = few
        c = cost[f]
        rhs = (-c).astype(bf16)
        primal = dot(full, rhs)
        h1 = dot(few, rhs)
        low, high = limits(geo, lim, f)
        t = jnp.minimum(jnp.maximum(primal, low), high) - c
        target[f] = t
        h2 = dot(few, t.astype(bf16))
        tall = jnp.concatenate([hot, jnp.zeros((LANES - THIN, K), bf16)], axis=0)
        square = lax.dot_general(few, tall, (((1,), (1,)), ((), ())), preferred_element_type=f32)
        r = rank[f]
        k = lax.div(sub[f], geo.S)
        square = pltpu.roll(square, r * Q, 1)
        row0 = jnp.zeros((1, LANES), f32)
        row1 = jnp.zeros((1, LANES), f32)
        for i in range(geo.Q2):
            moved = roll(square, i * geo.PR * Q)
            row0 = row0 + moved[i : i + 1]
            row1 = row1 + moved[geo.Q2 + i : geo.Q2 + i + 1]
        ident = jnp.where(f < live[0], sub[f] - k * geo.S + 1, 0).astype(f32)
        row0 = row0 + jnp.where(iota((1, LANES), 1) == geo.id_lane + r, ident, 0.0)
        meta[pl.ds(k, 1), :] = meta[pl.ds(k, 1), :] + row0
        meta[pl.ds(NB + k, 1), :] = meta[pl.ds(NB + k, 1), :] + row1
        at = base[f]
        for q in range(Q):
            stage1[pl.ds(at + geo.off(q), 1), :] = h1[q : q + 1]
            stage2[pl.ds(at + geo.off(q), 1), :] = h2[q : q + 1]
        return carry

    lax.fori_loop(0, F, body, 0)
    pack(geo, stage1, send, chunk, 0)
    pack(geo, stage2, send, chunk, X)
    for j in range(geo.G):
        for m in range(2):
            send[pl.ds(j * chunk + 2 * X + m, NB, stride=geo.G * chunk), :] = meta[
                m * NB : (m + 1) * NB
            ]


def solve(geo, f, iface, base, inverse, cost, lim, work, stage):
    at = base[f]
    for q in range(geo.Q):
        where = pl.ds(iface[f, q], 1)
        work[where, :] = work[where, :] + stage[pl.ds(at + geo.off(q), 1), :]
    primal = dot(inverse[f], work[...].astype(bf16))
    low, high = limits(geo, lim, f)
    return jnp.minimum(jnp.maximum(primal, low), high)


def feeder_steps(geo, steps, iface, base, inverse, cost, target, thin, lim, recv,
                 target_out, send, work, *stages):
    chunk_in = recv.shape[0] // geo.D
    chunk_out = steps * geo.X
    arrived, leaving = stages[:steps], stages[steps:]
    for s in range(steps):
        unpack(geo, recv, arrived[s], chunk_in, s * geo.X)
        leaving[s][...] = jnp.zeros_like(leaving[s])

    def body(f, carry):
        at = base[f]
        c = cost[f]
        work[...] = target[f]
        for s in range(steps):
            t = solve(geo, f, iface, base, inverse, cost, lim, work, arrived[s]) - c
            if s < steps - 1:
                work[...] = t
            h = dot(thin[f], t.astype(bf16))
            for q in range(geo.Q):
                leaving[s][pl.ds(at + geo.off(q), 1), :] = h[q : q + 1]
        target_out[f] = t
        return carry

    lax.fori_loop(0, geo.F, body, 0)
    for s in range(steps):
        pack(geo, leaving[s], send, chunk_out, s * geo.X)


def feeder_last(geo, iface, base, live, inverse, cost, target, lim, recv, out, work, stage):
    unpack(geo, recv, stage, recv.shape[0] // geo.D, geo.X)

    def body(f, carry):
        work[...] = target[f]
        anchor = solve(geo, f, iface, base, inverse, cost, lim, work, stage)
        out[f] = anchor * jnp.where(f < live[0], 1.0, 0.0)
        return carry

    lax.fori_loop(0, geo.F, body, 0)


def slice_parity(geo, shape):
    lane = iota(shape, 1)
    half = geo.RP * geo.L
    qp = jnp.where(lane >= half, 1, 0)
    inner = lane - qp * half
    rp = jnp.zeros(shape, i32)
    for i in range(1, geo.RP):
        rp = rp + jnp.where(inner >= i * geo.L, 1, 0)
    return qp, rp


def owner_setup(geo, slice_index, weight, aim, recv, coef, hot_t, hot, act, scaled, den, count):
    X, D, S, Q, Q2, R2, RP, PR = geo.X, geo.D, geo.S, geo.Q, geo.Q2, geo.R2, geo.RP, geo.PR
    chunk = 2 * X + 2
    metas = [recv[pl.ds(2 * X + m, D, stride=chunk), :] for m in range(2)]
    qp, rp = slice_parity(geo, (D, LANES))
    padded = metas[0]
    if D < LANES:
        padded = jnp.concatenate([padded, jnp.zeros((LANES - D, LANES), f32)], axis=0)
    turned = padded.T
    total = jnp.zeros((S, D), f32)
    for r2 in range(R2):
        live = jnp.zeros((D, LANES), f32)
        for p in range(RP):
            r = r2 * RP + p
            col = metas[0][:, geo.id_lane + r : geo.id_lane + r + 1]
            wide = jnp.broadcast_to(col, (D, LANES))
            live = jnp.where(rp == p, jnp.where(wide > 0.5, 1.0, 0.0), live)
            mine = (wide == (iota((D, LANES), 1) + 1).astype(f32)).astype(f32)
            hot[(p * R2 + r2) * D : (p * R2 + r2 + 1) * D, :] = mine[:, :S].astype(bf16)
            row = turned[geo.id_lane + r : geo.id_lane + r + 1, :D]
            theirs = (
                jnp.broadcast_to(row, (S, D)) == (iota((S, D), 0) + 1).astype(f32)
            ).astype(f32)
            total = total + theirs
            hot_t[r2, p * S : (p + 1) * S, :] = theirs.astype(bf16)
        act[r2 * D : (r2 + 1) * D, :] = live
    members = jnp.sum(total, axis=1, keepdims=True)
    w = jnp.zeros((S, LANES), f32)
    for s in range(S):
        w = jnp.where(iota((S, LANES), 0) == s, weight[s], w)
    members = jnp.broadcast_to(members, (S, LANES))
    den[...] = members + w
    qps, rps = slice_parity(geo, (S, LANES))
    count[...] = jnp.where(rps == 0, members, 0.0)
    lane = iota((S, LANES), 1)
    inner = lane - (qps * RP + rps) * geo.L
    index = inner + slice_index * geo.L
    for q2 in range(Q2):
        even = jnp.take_along_axis(aim[:, 2 * q2, :], index, axis=1)
        odd = jnp.take_along_axis(aim[:, 2 * q2 + 1, :], index, axis=1)
        scaled[:, q2 * LANES : (q2 + 1) * LANES] = w * jnp.where(qps == 0, even, odd)
    for par in range(2):
        for q2 in range(Q2):
            for q2p in range(Q2):
                for r2 in range(R2):
                    sides = []
                    for side in range(2):
                        q = 2 * q2 + side
                        other = 2 * q2p + (side if par == 0 else 1 - side)
                        sides.append((q // Q2, (q % Q2) * PR * Q + r2 * RP * Q + other))
                    idx = rp * Q + jnp.where(qp == 0, sides[0][1], sides[1][1])
                    if sides[0][0] == sides[1][0]:
                        value = jnp.take_along_axis(metas[sides[0][0]], idx, axis=1)
                    else:
                        value = jnp.where(
                            qp == 0,
                            jnp.take_along_axis(metas[sides[0][0]], idx, axis=1),
                            jnp.take_along_axis(metas[sides[1][0]], idx, axis=1),
                        )
                    coef[(par * Q2 + q2) * Q2 + q2p, r2 * D : (r2 + 1) * D, :] = value


def arrive(geo, recv, chunk, off):
    return [
        jnp.concatenate(
            [
                recv[pl.ds(off + q2 * geo.R2 + r2, geo.D, stride=chunk), :]
                for r2 in range(geo.R2)
            ],
            axis=0,
        )
        for q2 in range(geo.Q2)
    ]


def depart(geo, values, send, chunk, off):
    for q2 in range(geo.Q2):
        for r2 in range(geo.R2):
            send[pl.ds(off + q2 * geo.R2 + r2, geo.D, stride=chunk), :] = values[q2][
                r2 * geo.D : (r2 + 1) * geo.D
            ]


def split(x):
    high = x.astype(bf16)
    return high, (x - high.astype(f32)).astype(bf16)


def owner_step(geo, h, raised, dual, old, coef, hot_t, hot, act, scaled, den, count):
    D, S, Q2, R2, RP = geo.D, geo.S, geo.Q2, geo.R2, geo.RP
    n = R2 * D
    rows = list(h)
    if raised is not None:
        turned = [roll(v, geo.RP * geo.L) for v in raised]
        for q2 in range(Q2):
            acc = rows[q2]
            for q2p in range(Q2):
                acc = acc + coef[q2 * Q2 + q2p] * raised[q2p]
                acc = acc + coef[(Q2 + q2) * Q2 + q2p] * turned[q2p]
            rows[q2] = acc
    if dual is not None:
        rows = [b + u for b, u in zip(rows, dual)]
    high, low = split(jnp.concatenate(rows, axis=1))
    sums = None
    for r2 in range(R2):
        part = slice(r2 * D, (r2 + 1) * D)
        term = dot(hot_t[r2], high[part]) + dot(hot_t[r2], low[part])
        sums = term if sums is None else sums + term
    _, rps = slice_parity(geo, (S, LANES))
    fresh = []
    for q2 in range(Q2):
        cols = slice(q2 * LANES, (q2 + 1) * LANES)
        mine = sums[0:S, cols]
        for p in range(1, RP):
            mine = jnp.where(rps == p, sums[p * S : (p + 1) * S, cols], mine)
        whole = mine
        for s in range(1, RP):
            whole = whole + jnp.where(rps >= s, roll(mine, s * geo.L), 0.0)
            whole = whole + jnp.where(rps < RP - s, roll(mine, -s * geo.L), 0.0)
        fresh.append((whole + scaled[:, cols]) / den[...])
    high, low = split(jnp.concatenate(fresh, axis=1))
    back = dot(hot[...], high) + dot(hot[...], low)
    _, rpn = slice_parity(geo, (n, LANES))
    new_dual, new_raise = [], []
    moved = jnp.zeros((1, LANES), f32)
    for q2 in range(Q2):
        cols = slice(q2 * LANES, (q2 + 1) * LANES)
        own = back[0:n, cols]
        for p in range(1, RP):
            own = jnp.where(rpn == p, back[p * n : (p + 1) * n, cols], own)
        u = (rows[q2] - own) * act[...]
        new_dual.append(u)
        new_raise.append(PENALTY * (own - u))
        step = u if dual is None else u - dual[q2]
        moved = moved + jnp.sum(step * step, axis=0, keepdims=True)
    shifted = jnp.zeros((1, LANES), f32)
    for q2 in range(Q2):
        gap = fresh[q2] if old is None else fresh[q2] - old[q2]
        shifted = shifted + jnp.sum(count[...] * gap * gap, axis=0, keepdims=True)
    return new_dual, new_raise, fresh, moved, shifted


def read_list(geo, ref):
    return [ref[:, q2 * LANES : (q2 + 1) * LANES] for q2 in range(geo.Q2)]


def write_list(geo, ref, values):
    for q2 in range(geo.Q2):
        ref[:, q2 * LANES : (q2 + 1) * LANES] = values[q2]


def owner_first(geo, slice_index, weight, aim, recv,
                send, coef, hot_t, hot, act, scaled, den, count, dual, raised, old, norms):
    X = geo.X
    owner_setup(geo, slice_index[0], weight, aim, recv, coef, hot_t, hot, act, scaled, den, count)
    tables = (coef, hot_t, hot, act, scaled, den, count)
    chunk = 2 * X + 2
    h = arrive(geo, recv, chunk, 0)
    u, v, z, p0, d0 = owner_step(geo, h, None, None, None, *tables)
    depart(geo, v, send, 2 * X, 0)
    h = arrive(geo, recv, chunk, X)
    u, v, z, p1, d1 = owner_step(geo, h, v, u, z, *tables)
    depart(geo, v, send, 2 * X, X)
    write_list(geo, dual, u)
    write_list(geo, raised, v)
    write_list(geo, old, z)
    norms[...] = jnp.zeros_like(norms)
    for i, value in enumerate((p0, d0, p1, d1)):
        norms[i : i + 1] = value


def owner_middle(geo, first, recv, coef, hot_t, hot, act, scaled, den, count,
                 dual, raised, old, norms, send, dual_out, raised_out, old_out, norms_out):
    X = geo.X
    tables = (coef, hot_t, hot, act, scaled, den, count)
    u, v, z = read_list(geo, dual), read_list(geo, raised), read_list(geo, old)
    norms_out[...] = norms[...]
    for s in range(2):
        h = arrive(geo, recv, 2 * X, s * X)
        u, v, z, p, d = owner_step(geo, h, v, u, z, *tables)
        depart(geo, v, send, 2 * X, s * X)
        at = 2 * (first + s)
        norms_out[at : at + 1] = p
        norms_out[at + 1 : at + 2] = d
    write_list(geo, dual_out, u)
    write_list(geo, raised_out, v)
    write_list(geo, old_out, z)


def owner_last(geo, recv, coef, hot_t, hot, act, scaled, den, count,
               dual, raised, old, norms, send, agreed):
    X, S, RP = geo.X, geo.S, geo.RP
    tables = (coef, hot_t, hot, act, scaled, den, count)
    u, v, z = read_list(geo, dual), read_list(geo, raised), read_list(geo, old)
    h = arrive(geo, recv, X, 0)
    u, v, z, p, d = owner_step(geo, h, v, u, z, *tables)
    depart(geo, [PENALTY * x for x in u], send, X + 1, 0)
    at = 2 * (ITERS - 1)
    everything = norms[...]
    rows = everything.shape[0]
    row = iota((rows, LANES), 0)
    everything = jnp.where(row == at, p, everything)
    everything = jnp.where(row == at + 1, d, everything)
    sums = jnp.sum(everything, axis=1, keepdims=True)
    line = jnp.sum(jnp.where(row == iota((rows, LANES), 1), sums, 0.0), axis=0, keepdims=True)
    send[pl.ds(X, geo.D, stride=X + 1), :] = jnp.broadcast_to(line, (geo.D, LANES))
    part = S // RP
    _, rps = slice_parity(geo, (part, LANES))
    for q2 in range(geo.Q2):
        value = z[q2][0:part]
        for i in range(1, RP):
            value = jnp.where(rps == i, z[q2][i * part : (i + 1) * part], value)
        agreed[q2 * part : (q2 + 1) * part, :] = value


def finish(geo, base, recv, agreed, duals, consensus, norms, stage):
    X, S, RP, G, L = geo.X, geo.S, geo.RP, geo.G, geo.L
    unpack(geo, recv, stage, X + 1, 0)

    def body(f, carry):
        at = base[f]
        for q in range(geo.Q):
            duals[f, q : q + 1, :] = stage[pl.ds(at + geo.off(q), 1), :]
        return carry

    lax.fori_loop(0, geo.F, body, 0)
    part = S // RP
    n = geo.Q2 * part
    for q2 in range(geo.Q2):
        sides = [agreed[j * n + q2 * part : j * n + (q2 + 1) * part, :] for j in range(G)]
        for qp in range(2):
            for rp in range(RP):
                acc = None
                for j in range(G):
                    v = roll(sides[j], (j - (qp * RP + rp)) * L)
                    acc = v if acc is None else jnp.where(group_mask((part, LANES), j, L), v, acc)
                consensus[rp * part : (rp + 1) * part, 2 * q2 + qp, :] = acc
    line = jnp.sum(recv[pl.ds(X, geo.D, stride=X + 1), :], axis=0, keepdims=True)
    line = jnp.sqrt(line)
    lane = iota((8, LANES), 1)
    wide = jnp.broadcast_to(line, (8, LANES))
    table = jnp.zeros((8, LANES), f32)
    for i in range(ITERS):
        table = jnp.where(iota((8, LANES), 0) == i, roll(wide, -2 * i), table)
    table = jnp.where(lane == 1, PENALTY * table, table)
    norms[...] = table[:ITERS, :2]


VM = pltpu.VMEM
SM = pltpu.SMEM


def call(body, args, ins, outs, scratch=(), name=None):
    specs = [pl.BlockSpec(memory_space=s) for s in ins]
    return pl.pallas_call(
        body,
        in_specs=specs,
        out_specs=[pl.BlockSpec(memory_space=s) for _, _, s in outs],
        out_shape=[jax.ShapeDtypeStruct(shape, dtype) for shape, dtype, _ in outs],
        scratch_shapes=list(scratch),
        compiler_params=pltpu.CompilerParams(vmem_limit_bytes=40 << 20),
        name=name,
    )(*args)


def shards(
    n_sub,
    n_fdr,
    inverse,
    cost,
    lower_limit,
    upper_limit,
    iface_rows,
    substation_of,
    live_count,
    reserve_weight,
    reserve_target,
):
    slots, rows, scen = cost.shape
    geo = Geometry(slots, rows, iface_rows.shape[1], scen, reserve_weight.shape[0], n_sub, n_fdr)
    F, K, Q, C, S, D, X = geo.F, geo.K, geo.Q, geo.C, geo.S, geo.D, geo.X
    R2, RP, Q2 = geo.R2, geo.RP, geo.Q2
    n, wide = R2 * D, Q2 * LANES

    def swap(x):
        y = x.reshape(D, 1, x.shape[0] // D * LANES)
        y = lax.all_to_all(y, ("sub", "fdr"), split_axis=0, concat_axis=0, tiled=True)
        return y.reshape(x.shape)

    stage = pltpu.VMEM((geo.stage_rows, LANES), f32)
    work = pltpu.VMEM((K, LANES), f32)
    slice_index = lax.axis_index("fdr").astype(i32).reshape(1)

    target, thin, lim, base, send = call(
        functools.partial(feeder_first, geo),
        (iface_rows, substation_of, live_count, inverse, cost, lower_limit, upper_limit),
        (SM, SM, SM, VM, VM, VM, VM),
        (
            ((F, K, C), f32, VM),
            ((F, THIN, K), bf16, VM),
            ((K, LANES), f32, VM),
            ((F,), i32, SM),
            ((D * (2 * X + 2), LANES), f32, VM),
        ),
        (stage, stage, pltpu.VMEM((2 * geo.NB, LANES), f32), pltpu.SMEM((geo.NB,), i32),
         pltpu.SMEM((F,), i32)),
        "feeder_first",
    )
    state = (
        ((n, wide), f32, VM),
        ((n, wide), f32, VM),
        ((S, wide), f32, VM),
        ((16, LANES), f32, VM),
    )
    out = call(
        functools.partial(owner_first, geo),
        (slice_index, reserve_weight, reserve_target, swap(send)),
        (SM, SM, VM, VM),
        (
            ((D * 2 * X, LANES), f32, VM),
            ((2 * Q2 * Q2, n, LANES), f32, VM),
            ((R2, RP * S, D), bf16, VM),
            ((RP * n, S), bf16, VM),
            ((n, LANES), f32, VM),
            ((S, wide), f32, VM),
            ((S, LANES), f32, VM),
            ((S, LANES), f32, VM),
        )
        + state,
        (),
        "owner_first",
    )
    send, tables, memory = out[0], out[1:8], out[8:]
    for first in range(2, ITERS - 1, 2):
        recv = swap(send)
        target, send = call(
            functools.partial(feeder_steps, geo, 2),
            (iface_rows, base, inverse, cost, target, thin, lim, recv),
            (SM, SM, VM, VM, VM, VM, VM, VM),
            (((F, K, C), f32, VM), ((D * 2 * X, LANES), f32, VM)),
            (work, stage, stage, stage, stage),
            "feeder_steps",
        )
        out = call(
            functools.partial(owner_middle, geo, first),
            (swap(send), *tables, *memory),
            (VM,) * 12,
            (((D * 2 * X, LANES), f32, VM),) + state,
            (),
            "owner_middle",
        )
        send, memory = out[0], out[1:]
    recv = swap(send)
    target, send = call(
        functools.partial(feeder_steps, geo, 1),
        (iface_rows, base, inverse, cost, target, thin, lim, recv),
        (SM, SM, VM, VM, VM, VM, VM, VM),
        (((F, K, C), f32, VM), ((D * X, LANES), f32, VM)),
        (work, stage, stage),
        "feeder_ahead",
    )
    (setpoints,) = call(
        functools.partial(feeder_last, geo),
        (iface_rows, base, live_count, inverse, cost, target, lim, recv),
        (SM, SM, SM, VM, VM, VM, VM, VM),
        (((F, K, C), f32, VM),),
        (work, stage),
        "feeder_last",
    )
    send, agreed = call(
        functools.partial(owner_last, geo),
        (swap(send), *tables, *memory),
        (VM,) * 12,
        (((D * (X + 1), LANES), f32, VM), ((Q2 * S // RP, LANES), f32, VM)),
        (),
        "owner_last",
    )
    gathered = lax.all_gather(agreed, "fdr", axis=0, tiled=True)
    duals, consensus, norms = call(
        functools.partial(finish, geo),
        (base, swap(send), gathered),
        (SM, VM, VM),
        (((F, Q, C), f32, VM), ((S, Q, C), f32, VM), ((ITERS, 2), f32, VM)),
        (stage,),
        "finish",
    )
    return duals, consensus, norms, setpoints


def solution(mesh):
    placed = (
        P(("sub", "fdr"), None, None),
        P(("sub", "fdr"), None, None),
        P(("sub", "fdr"), None),
        P(("sub", "fdr"), None),
        P(("sub", "fdr"), None),
        P(("sub", "fdr")),
        P(("sub", "fdr")),
        P("sub"),
        P("sub", None, None),
    )
    return jax.shard_map(
        functools.partial(shards, mesh.shape["sub"], mesh.shape["fdr"]),
        mesh=mesh,
        in_specs=placed,
        out_specs=(
            P(("sub", "fdr"), None, None),
            P("sub", None, None),
            P(),
            P(("sub", "fdr"), None, None),
        ),
        check_vma=False,
    )
```

time: 617 us -> 177 us (0.29)
  waiting for transfers between devices: 156 us -> 12 us
  other arithmetic: 121 us -> 0 us
  blocking collectives: 129 us -> 56.3 us
  Pallas kernels: 0 us -> 70.1 us
  local copies, waits for them, and re-layouts: 91.1 us -> 26.3 us
  matrix products: 56.4 us -> 0 us
  starting transfers between devices: 41.1 us -> 9.9 us
  between operations: 18.1 us -> 1.4 us
    psum x5 -> x0, waiting for transfers between devices: 147 us -> none  [shards(): collected = lax.psum(block_sums, 'fdr')]
    scatter-add x5 -> x0, other arithmetic: 100 us -> none  [shards(): right_side = (anchor - cost).at[feeder_index, iface_rows].add(penalty * (...]
    psum x2 -> x0, blocking collectives: 84 us -> none  [the longest x1 43.2 us: shards(): primal_sum, dual_sum = lax.psum((primal_local, dual_local), ('sub', 'fdr'))]
    pallas_call x0 -> x8, Pallas kernels: none -> 70.1 us  [call(): pl.pallas_call(body, in_specs=specs, out_specs=[pl.BlockSpec(memory_space...]
    dot_general x25 -> x0, matrix products: 56.4 us -> none  [the longest x5 46 us: shards(): jnp.einsum('fkj,fjs->fks', inverse, right_side, preferred_element_type=jn...]
    all_to_all x7 -> x2, starting transfers between devices: 40.7 us -> 9.9 us  [swap(): lax.all_to_all(y, ('sub', 'fdr'), split_axis=0, concat_axis=0, tiled=True)]
    dot_general x5 -> x0, local copies, waits for them, and re-layouts: 27.9 us -> none  [shards(): jnp.einsum('fkj,fjs->fks', inverse, right_side, preferred_element_type=jn...]
    sub x6 -> x0, local copies, waits for them, and re-layouts: 23.1 us -> none  [the longest x4 22.3 us: shards(): anchor - cost]
  transfers between devices with their start and end apart: 12 -> 2, of which waited for: 9 -> 1; matrix products, arithmetic and copies ran while one was open for 13% -> 0% of each run, Pallas kernels for 0% -> 6%
where the time goes in v1:
time: 177 us; the launch traced here: 176 us
  Pallas kernels  70.1 us (40%)
  blocking collectives  56.3 us (32%)
  local copies, waits for them, and re-layouts  26.3 us (15%)
  waiting for transfers between devices  12 us (7%)
  starting transfers between devices  9.9 us (6%)
    pallas_call x8, Pallas kernels, call(): pl.pallas_call(body, in_specs=specs, out_specs=[pl.BlockSpec(memory_space...  70.1 us
    all_to_all x4, blocking collectives, swap(): lax.all_to_all(y, ('sub', 'fdr'), split_axis=0, concat_axis=0, tiled=True)  51 us
    unnamed x37, local copies, waits for them, and re-layouts  26.3 us
    all_to_all x2, waiting for transfers between devices, swap(): lax.all_to_all(y, ('sub', 'fdr'), split_axis=0, concat_axis=0, tiled=True)  12 us
    all_to_all x2, starting transfers between devices, swap(): lax.all_to_all(y, ('sub', 'fdr'), split_axis=0, concat_axis=0, tiled=True)  9.9 us
    all_gather x1, blocking collectives, shards(): gathered = lax.all_gather(agreed, 'fdr', axis=0, tiled=True)  5.31 us
  transfers between devices with their start and end apart: 2, of which 1 were waited for; matrix products, arithmetic and copies ran while one was open for 0% of the time, Pallas kernels for 6%

profile of v1, /device:TPU:0, one launch (start us, length us, event | category | flops | bytes accessed | tf_op | source)
XLA Modules:
  0.0 176.0 jit_solution(15177819394218699528)
XLA Ops:
  1.3 0.8 copy.21.iface
  2.0 0.0 copy-start
  2.0 2.2 %copy-done = bf16[32,256,256]{2,1,0:T(8,128)(2,1)S(1)} copy-done((bf16[32,256,256]{2,1,0:T(8,128)(2,1)S(1)}, bf16[32,256,256]{2,1,0:T(8,128)(2,1)}, u32[]{:S(2)}) %copy-start) | copy-done | bytes 4194328
  4.2 0.0 copy-start.4
  4.2 2.2 %copy-done.4 = f32[32,256,128]{2,1,0:T(8,128)S(1)} copy-done((f32[32,256,128]{2,1,0:T(8,128)S(1)}, f32[32,256,128]{2,1,0:T(8,128)}, u32[]{:S(2)}) %copy-start.4) | copy-done | bytes 4194328
  6.4 0.0 copy-start.11
  6.4 0.8 copy-done.11
  7.2 0.0 copy-start.12
  7.2 0.8 copy-done.12
  7.9 0.0 copy-start.13
  7.9 0.7 copy-done.13
  8.6 0.0 copy-start.15
  8.6 17.4 %feeder_first.1 = (f32[32,256,128]{2,1,0:T(8,128)S(1)}, bf16[32,16,256]{2,1,0:T(8,128)(2,1)S(1)}, f32[256,128]{1,0:T(8,128)S(1)}, s32[32]{0:T(128)S(1)}, f32[640,128]{1,0:T(8,128)}) custom-call(s32[32,6]{1,0:T(8,128)S(1)} %copy.21.iface, s32[32]{0:T(128)S(1)} %copy-done.13, s32[1]{0:T(128)S(6)} %copy.35.live, bf16[32,256,256]{2,1,0:T(8,128)(2,1)S(1)} %copy-done, ...), custom_call_target="tpu_custom_call" | custom-call | tf_op jit(solution)/shard_map/feeder_first/pallas_call | solution.py:485
  26.0 0.0 copy-start.7
  26.1 2.0 %copy-done.7 = f32[32,256,128]{2,1,0:T(8,128)} copy-done((f32[32,256,128]{2,1,0:T(8,128)}, f32[32,256,128]{2,1,0:T(8,128)S(1)}, u32[]{:S(2)}) %copy-start.7) | copy-done | bytes 4194328
  28.1 7.3 %all-to-all-start = ((f32[32,1,2560]{2,1,0:T(1,128)}), f32[32,1,2560]{2,1,0:T(1,128)S(1)}, u32[]{:S(2)}, u32[]{:S(2)}) async-start(f32[32,1,2560]{2,1,0:T(1,128)} %bitcast.1), calls=%async_computation | async-start | bytes 655360 | tf_op jit(solution)/shard_map/all_to_all | solution.py:517
  35.4 0.0 copy-done.15
  35.4 0.1 copy.23.aim
  35.5 12.0 %all-to-all-done = f32[32,1,2560]{2,1,0:T(1,128)S(1)} async-done(((f32[32,1,2560]{2,1,0:T(1,128)}), f32[32,1,2560]{2,1,0:T(1,128)S(1)}, u32[]{:S(2)}, u32[]{:S(2)}) %all-to-all-start) | async-done | bytes 327712 | tf_op jit(solution)/shard_map/all_to_all | solution.py:517
  47.4 0.0 copy-done.14
  47.4 2.0 %owner_first.1 = (f32[576,128]{1,0:T(8,128)S(1)}, f32[18,96,128]{2,1,0:T(8,128)S(1)}, bf16[3,64,32]{2,1,0:T(8,128)(2,1)S(1)}, bf16[192,32]{1,0:T(8,128)(2,1)S(1)...) custom-call(s32[1]{0:T(128)} %bitcast.slice_index, ...), custom_call_target="tpu_custom_call" | custom-call | tf_op jit(solution)/shard_map/owner_first/pallas_call | solution.py:485
  49.5 13.5 %all_to_all.30 = f32[32,1,2304]{2,1,0:T(1,128)S(1)} all-to-all(f32[32,1,2304]{2,1,0:T(1,128)S(1)} %bitcast.20), channel_id=1, replica_groups=mesh['sub'=8,'fdr'=4] {'sub','fdr'}, dimensions={0} | all-to-all | bytes 589824 | tf_op jit(solution)/shard_map/all_to_all | solution.py:517
  63.0 2.2 %copy-done.1 = bf16[32,256,256]{2,1,0:T(8,128)(2,1)S(1)} copy-done((bf16[32,256,256]{2,1,0:T(8,128)(2,1)S(1)}, bf16[32,256,256]{2,1,0:T(8,128)(2,1)}, u32[]{:S(2)}) %copy-start.1) | copy-done | bytes 4194328
  65.2 2.2 %copy-done.5 = f32[32,256,128]{2,1,0:T(8,128)S(1)} copy-done((f32[32,256,128]{2,1,0:T(8,128)S(1)}, f32[32,256,128]{2,1,0:T(8,128)}, u32[]{:S(2)}) %copy-start.5) | copy-done | bytes 4194328
  67.4 22.4 %feeder_steps.1 = (f32[32,256,128]{2,1,0:T(8,128)S(1)}, f32[576,128]{1,0:T(8,128)S(1)}) custom-call(s32[32,6]{1,0:T(8,128)S(1)} %copy.21.iface, s32[32]{0:T(128)S(1)} %get-tuple-element.35.base, bf16[32,256,256]{2,1,0:T(8,128)(2,1)S(1)} %copy-done.1, f32[32,256,128]{2,1,0:T(8,128)S(1)} %copy-done.5, f32[32,256,128]{2,1,0:T(8,128)} %copy-done.7, ...), custom_call_target="tpu_custom_call" | custom-call | tf_op jit(solution)/shard_map/feeder_steps/pallas_call | solution.py:485
  89.8 0.0 copy-start.10
  89.8 2.0 %copy-done.10 = f32[32,256,128]{2,1,0:T(8,128)} copy-done((f32[32,256,128]{2,1,0:T(8,128)}, f32[32,256,128]{2,1,0:T(8,128)S(1)}, u32[]{:S(2)}) %copy-start.10) | copy-done | bytes 4194328
  91.8 13.5 %all_to_all.31 = f32[32,1,2304]{2,1,0:T(1,128)S(1)} all-to-all(f32[32,1,2304]{2,1,0:T(1,128)S(1)} %bitcast.22), channel_id=1, replica_groups=mesh['sub'=8,'fdr'=4] {'sub','fdr'}, dimensions={0} | all-to-all | bytes 589824 | tf_op jit(solution)/shard_map/all_to_all | solution.py:517
  105.3 1.3 owner_middle.1
  106.6 13.5 %all_to_all.32 = f32[32,1,2304]{2,1,0:T(1,128)S(1)} all-to-all(f32[32,1,2304]{2,1,0:T(1,128)S(1)} %bitcast.21), channel_id=1, replica_groups=mesh['sub'=8,'fdr'=4] {'sub','fdr'}, dimensions={0} | all-to-all | bytes 589824 | tf_op jit(solution)/shard_map/all_to_all | solution.py:517
  120.1 0.0 copy-done.2
  120.1 14.3 %feeder_ahead.1 = (f32[32,256,128]{2,1,0:T(8,128)S(1)}, f32[288,128]{1,0:T(8,128)S(1)}) custom-call(s32[32,6]{1,0:T(8,128)S(1)} %copy.21.iface, s32[32]{0:T(128)S(1)} %get-tuple-element.35.base, bf16[32,256,256]{2,1,0:T(8,128)(2,1)S(1)} %copy-done.2, f32[32,256,128]{2,1,0:T(8,128)S(1)} %copy-done.5, f32[32,256,128]{2,1,0:T(8,128)} %copy-done.10, ...), custom_call_target="tpu_custom_call" | custom-call | tf_op jit(solution)/shard_map/feeder_ahead/pallas_call | solution.py:485
  134.3 0.0 copy-start.8
  134.4 2.0 %copy-done.8 = f32[32,256,128]{2,1,0:T(8,128)} copy-done((f32[32,256,128]{2,1,0:T(8,128)}, f32[32,256,128]{2,1,0:T(8,128)S(1)}, u32[]{:S(2)}) %copy-start.8) | copy-done | bytes 4194328
  136.4 10.5 %all_to_all.33 = f32[32,1,1152]{2,1,0:T(1,128)S(1)} all-to-all(f32[32,1,1152]{2,1,0:T(1,128)S(1)} %bitcast.23), channel_id=1, replica_groups=mesh['sub'=8,'fdr'=4] {'sub','fdr'}, dimensions={0} | all-to-all | bytes 294912 | tf_op jit(solution)/shard_map/all_to_all | solution.py:517
  146.8 1.4 owner_last.1
  148.3 2.6 %all-to-all-start.5 = ((f32[32,1,1280]{2,1,0:T(1,128)}), f32[32,1,1280]{2,1,0:T(1,128)S(1)}, u32[]{:S(2)}, u32[]{:S(2)}) async-start(f32[32,1,1280]{2,1,0:T(1,128)} %bitcast.11), calls=%async_computation.5 | async-start | bytes 327680 | tf_op jit(solution)/shard_map/all_to_all | solution.py:517
  150.9 0.0 copy-start.3
  150.9 2.2 %copy-done.3 = bf16[32,256,256]{2,1,0:T(8,128)(2,1)S(1)} copy-done((bf16[32,256,256]{2,1,0:T(8,128)(2,1)S(1)}, bf16[32,256,256]{2,1,0:T(8,128)(2,1)}, u32[]{:S(2)}) %copy-start.3) | copy-done | bytes 4194328
  153.1 2.2 %copy-done.6 = f32[32,256,128]{2,1,0:T(8,128)S(1)} copy-done((f32[32,256,128]{2,1,0:T(8,128)S(1)}, f32[32,256,128]{2,1,0:T(8,128)}, u32[]{:S(2)}) %copy-start.6) | copy-done | bytes 4194328
  155.2 2.2 %copy-done.9 = f32[32,256,128]{2,1,0:T(8,128)S(1)} copy-done((f32[32,256,128]{2,1,0:T(8,128)S(1)}, f32[32,256,128]{2,1,0:T(8,128)}, u32[]{:S(2)}) %copy-start.9) | copy-done | bytes 4194328
  157.4 10.2 %feeder_last.1 = f32[32,256,128]{2,1,0:T(8,128)} custom-call(s32[32,6]{1,0:T(8,128)S(1)} %copy.21.iface, s32[32]{0:T(128)S(1)} %get-tuple-element.35.base, s32[1]{0:T(128)S(6)} %copy.35.live, bf16[32,256,256]{2,1,0:T(8,128)(2,1)S(1)} %copy-done.3, f32[32,256,128]{2,1,0:T(8,128)S(1)} %copy-done.6, f32[32,256,128]{2,1,0:T(8,128)S(1)} %copy-done.9, ...), custom_call_target="tpu_custom_call" | custom-call | tf_op jit(solution)/shard_map/feeder_last/pallas_call | solution.py:485
  167.6 5.3 %all_gather.3.agreed = f32[192,128]{1,0:T(8,128)S(1)} all-gather(f32[48,128]{1,0:T(8,128)S(1)} %get-tuple-element.61), channel_id=1, replica_groups=mesh['sub'=8,'fdr'=4] {'fdr'}, dimensions={0}, use_global_device_ids=true | all-gather | bytes 122880 | tf_op jit(solution)/shard_map/all_gather | solution.py:608
  172.9 0.0 all-to-all-done.5
  172.9 1.1 finish.1
  174.0 0.7 copy.32
  174.7 0.6 copy.34
  175.3 0.7 copy.33
  (6 shorter events, 0.0 us)
Async XLA Ops:
  2.0 2.2 %copy-start = (bf16[32,256,256]{2,1,0:T(8,128)(2,1)S(1)}, bf16[32,256,256]{2,1,0:T(8,128)(2,1)}, u32[]{:S(2)}) copy-start(bf16[32,256,256]{2,1,0:T(8,128)(2,1)} %inverse.7) | copy-start | bytes 12582916
  4.2 2.2 %copy-start.4 = (f32[32,256,128]{2,1,0:T(8,128)S(1)}, f32[32,256,128]{2,1,0:T(8,128)}, u32[]{:S(2)}) copy-start(f32[32,256,128]{2,1,0:T(8,128)} %cost.7) | copy-start | bytes 12582916
  6.4 0.8 copy-start.11
  7.2 0.8 copy-start.12
  7.9 0.7 copy-start.13
  8.6 26.8 %copy-start.15 = (f32[32,6,128]{2,0,1:T(8,128)S(1)}, f32[32,6,128]{2,0,1:T(8,128)}, u32[]{:S(2)}) copy-start(f32[32,6,128]{2,0,1:T(8,128)} %param.17) | copy-start | bytes 294916
  8.6 38.8 %copy-start.14 = (f32[32]{0:T(128)S(1)}, f32[32]{0:T(128)}, u32[]{:S(2)}) copy-start(f32[32]{0:T(128)} %weight.1) | copy-start | bytes 388
  26.0 2.0 %copy-start.7 = (f32[32,256,128]{2,1,0:T(8,128)}, f32[32,256,128]{2,1,0:T(8,128)S(1)}, u32[]{:S(2)}) copy-start(f32[32,256,128]{2,1,0:T(8,128)S(1)} %get-tuple-element.36.target) | copy-start | bytes 12582916
  28.1 19.4 %all-to-all-start = ((f32[32,1,2560]{2,1,0:T(1,128)}), f32[32,1,2560]{2,1,0:T(1,128)S(1)}, u32[]{:S(2)}, u32[]{:S(2)}) async-start(f32[32,1,2560]{2,1,0:T(1,128)} %bitcast.1), calls=%async_computation | async-start | bytes 655360 | tf_op jit(solution)/shard_map/all_to_all | solution.py:517
  63.0 2.2 %copy-start.1 = (bf16[32,256,256]{2,1,0:T(8,128)(2,1)S(1)}, bf16[32,256,256]{2,1,0:T(8,128)(2,1)}, u32[]{:S(2)}) copy-start(bf16[32,256,256]{2,1,0:T(8,128)(2,1)} %inverse.7) | copy-start | bytes 12582916
  65.2 2.2 %copy-start.5 = (f32[32,256,128]{2,1,0:T(8,128)S(1)}, f32[32,256,128]{2,1,0:T(8,128)}, u32[]{:S(2)}) copy-start(f32[32,256,128]{2,1,0:T(8,128)} %cost.7) | copy-start | bytes 12582916
  67.4 52.7 %copy-start.2 = (bf16[32,256,256]{2,1,0:T(8,128)(2,1)S(1)}, bf16[32,256,256]{2,1,0:T(8,128)(2,1)}, u32[]{:S(2)}) copy-start(bf16[32,256,256]{2,1,0:T(8,128)(2,1)} %inverse.7) | copy-start | bytes 12582916
  89.8 2.0 %copy-start.10 = (f32[32,256,128]{2,1,0:T(8,128)}, f32[32,256,128]{2,1,0:T(8,128)S(1)}, u32[]{:S(2)}) copy-start(f32[32,256,128]{2,1,0:T(8,128)S(1)} %get-tuple-element.41.target) | copy-start | bytes 12582916
  134.3 2.0 %copy-start.8 = (f32[32,256,128]{2,1,0:T(8,128)}, f32[32,256,128]{2,1,0:T(8,128)S(1)}, u32[]{:S(2)}) copy-start(f32[32,256,128]{2,1,0:T(8,128)S(1)} %get-tuple-element.65.target) | copy-start | bytes 12582916
  148.3 24.7 %all-to-all-start.5 = ((f32[32,1,1280]{2,1,0:T(1,128)}), f32[32,1,1280]{2,1,0:T(1,128)S(1)}, u32[]{:S(2)}, u32[]{:S(2)}) async-start(f32[32,1,1280]{2,1,0:T(1,128)} %bitcast.11), calls=%async_computation.5 | async-start | bytes 327680 | tf_op jit(solution)/shard_map/all_to_all | solution.py:517
  150.9 2.2 %copy-start.3 = (bf16[32,256,256]{2,1,0:T(8,128)(2,1)S(1)}, bf16[32,256,256]{2,1,0:T(8,128)(2,1)}, u32[]{:S(2)}) copy-start(bf16[32,256,256]{2,1,0:T(8,128)(2,1)} %inverse.7) | copy-start | bytes 12582916
  153.1 2.2 %copy-start.6 = (f32[32,256,128]{2,1,0:T(8,128)S(1)}, f32[32,256,128]{2,1,0:T(8,128)}, u32[]{:S(2)}) copy-start(f32[32,256,128]{2,1,0:T(8,128)} %cost.7) | copy-start | bytes 12582916
  155.2 2.2 %copy-start.9 = (f32[32,256,128]{2,1,0:T(8,128)S(1)}, f32[32,256,128]{2,1,0:T(8,128)}, u32[]{:S(2)}) copy-start(f32[32,256,128]{2,1,0:T(8,128)} %copy-done.8) | copy-start | bytes 12582916

commit v2 on v1

--- a/solution.py
+++ b/solution.py
@@ -11,6 +11,7 @@
 PENALTY = 2.0
 LANES = 128
 THIN = 16
+GROUP = 4
 
 f32 = jnp.float32
 bf16 = jnp.bfloat16
@@ -90,15 +91,43 @@
 
 
 def limits(geo, lim, f):
-    low = jnp.take_along_axis(lim[...], jnp.full((geo.K, LANES), f, i32), axis=1)
-    high = jnp.take_along_axis(lim[...], jnp.full((geo.K, LANES), f + geo.F, i32), axis=1)
+    table = lim[...]
+    low = jnp.take_along_axis(table, jnp.full((geo.K, LANES), f, i32), axis=1)
+    high = jnp.take_along_axis(table, jnp.full((geo.K, LANES), f + geo.F, i32), axis=1)
     return low, high
 
 
+def clip(x, low, high):
+    return jnp.minimum(jnp.maximum(x, low), high)
+
+
+def moves(pairs, sems, group):
+    count = pairs[0][0].shape[0] // group
+
+    def one(i, c):
+        src, dst = pairs[i]
+        part = pl.ds(c * group, group)
+        return pltpu.make_async_copy(src.at[part], dst.at[part], sems.at[i, c])
+
+    return count, one
+
+
+def pick(work, iface, f, q):
+    return work[pl.ds(iface[q, f], 1), :]
+
+
 def feeder_first(geo, iface, sub, live, inverse, cost, lower, upper,
-                 target, thin, lim, base, send, stage1, stage2, meta, count, rank):
+                 rounded, kept, lim, base, send,
+                 inv, price, out, sems, out_sems,
+                 stage1, stage2, meta, count, rank, *works):
     F, K, Q, NB, X = geo.F, geo.K, geo.Q, geo.NB, geo.X
     chunk = 2 * X + 2
+    bound, square, left, ahead = (works[i * GROUP : (i + 1) * GROUP] for i in range(4))
+    groups, load = moves(((inverse, inv), (cost, price)), sems, GROUP)
+    _, store = moves(((out, rounded),), out_sems, GROUP)
+    for c in range(groups):
+        for i in range(2):
+            load(i, c).start()
     for k in range(NB):
         count[k] = 0
 
@@ -118,46 +147,53 @@
     stage1[...] = jnp.zeros_like(stage1)
     stage2[...] = jnp.zeros_like(stage2)
     meta[...] = jnp.zeros_like(meta)
-
-    def body(f, carry):
-        row = iota((THIN, K), 0)
-        chosen = jnp.full((THIN, K), -1, i32)
-        for q in range(Q):
-            chosen = jnp.where(row == q, iface[f, q], chosen)
-        hot = (iota((THIN, K), 1) == chosen).astype(f32).astype(bf16)
-        full = inverse[f]
-        few = dot(hot, full).astype(bf16)
-        thin[f] = few
-        c = cost[f]
-        rhs = (-c).astype(bf16)
-        primal = dot(full, rhs)
-        h1 = dot(few, rhs)
-        low, high = limits(geo, lim, f)
-        t = jnp.minimum(jnp.maximum(primal, low), high) - c
-        target[f] = t
-        h2 = dot(few, t.astype(bf16))
-        tall = jnp.concatenate([hot, jnp.zeros((LANES - THIN, K), bf16)], axis=0)
-        square = lax.dot_general(few, tall, (((1,), (1,)), ((), ())), preferred_element_type=f32)
-        r = rank[f]
-        k = lax.div(sub[f], geo.S)
-        square = pltpu.roll(square, r * Q, 1)
-        row0 = jnp.zeros((1, LANES), f32)
-        row1 = jnp.zeros((1, LANES), f32)
-        for i in range(geo.Q2):
-            moved = roll(square, i * geo.PR * Q)
-            row0 = row0 + moved[i : i + 1]
-            row1 = row1 + moved[geo.Q2 + i : geo.Q2 + i + 1]
-        ident = jnp.where(f < live[0], sub[f] - k * geo.S + 1, 0).astype(f32)
-        row0 = row0 + jnp.where(iota((1, LANES), 1) == geo.id_lane + r, ident, 0.0)
-        meta[pl.ds(k, 1), :] = meta[pl.ds(k, 1), :] + row0
-        meta[pl.ds(NB + k, 1), :] = meta[pl.ds(NB + k, 1), :] + row1
-        at = base[f]
-        for q in range(Q):
-            stage1[pl.ds(at + geo.off(q), 1), :] = h1[q : q + 1]
-            stage2[pl.ds(at + geo.off(q), 1), :] = h2[q : q + 1]
+    kept[...] = jnp.zeros_like(kept)
+    lane = iota((1, LANES), 1)
+    third = jnp.zeros((1, LANES), i32)
+    for i in range(1, geo.Q2 + 1):
+        third = third + jnp.where(lane >= i * geo.PR * Q, 1, 0)
+    within = lane - third * (geo.PR * Q)
+
+    def body(c, carry):
+        for i in range(2):
+            load(i, c).wait()
+        fs = [c * GROUP + u for u in range(GROUP)]
+        for u, f in enumerate(fs):
+            at = within - rank[f] * Q
+            chosen = jnp.full((1, LANES), -1, i32)
+            for q in range(Q):
+                chosen = jnp.where((at == q) & (third < geo.Q2), iface[q, f], chosen)
+            hot = (iota((K, LANES), 0) == jnp.broadcast_to(chosen, (K, LANES))).astype(f32)
+            price_u = price[f]
+            both = dot(inv[f], jnp.concatenate([-price_u, hot], axis=1).astype(bf16))
+            primal = both[:, :LANES]
+            bound[u][...] = primal
+            square[u][...] = both[:, LANES:]
+            low, high = limits(geo, lim, f)
+            t = clip(primal, low, high) - price_u
+            left[u][...] = t
+            t = t.astype(bf16)
+            out[f] = t
+            ahead[u][...] = dot(inv[f], t)
+        store(0, c).start()
+        for u, f in enumerate(fs):
+            k = lax.div(sub[f], geo.S)
+            ident = jnp.where(f < live[0], sub[f] - k * geo.S + 1, 0).astype(f32)
+            lines = [jnp.where(lane == geo.id_lane + rank[f], ident, 0.0),
+                     jnp.zeros((1, LANES), f32)]
+            at = base[f]
+            for q in range(Q):
+                m, i = divmod(q, geo.Q2)
+                lines[m] = lines[m] + jnp.where(third == i, pick(square[u], iface, f, q), 0.0)
+                stage1[pl.ds(at + geo.off(q), 1), :] = pick(bound[u], iface, f, q)
+                stage2[pl.ds(at + geo.off(q), 1), :] = pick(ahead[u], iface, f, q)
+                kept[f, q : q + 1, :] = pick(left[u], iface, f, q)
+            for m in range(2):
+                spot = pl.ds(m * NB + k, 1)
+                meta[spot, :] = meta[spot, :] + lines[m]
         return carry
 
-    lax.fori_loop(0, F, body, 0)
+    lax.fori_loop(0, groups, body, 0)
     pack(geo, stage1, send, chunk, 0)
     pack(geo, stage2, send, chunk, X)
     for j in range(geo.G):
@@ -165,56 +201,81 @@
             send[pl.ds(j * chunk + 2 * X + m, NB, stride=geo.G * chunk), :] = meta[
                 m * NB : (m + 1) * NB
             ]
-
-
-def solve(geo, f, iface, base, inverse, cost, lim, work, stage):
+    for c in range(groups):
+        store(0, c).wait()
+
+
+def raise_rows(geo, f, iface, base, rows, work, stage):
     at = base[f]
+    rows = [rows[q] + stage[pl.ds(at + geo.off(q), 1), :] for q in range(geo.Q)]
     for q in range(geo.Q):
-        where = pl.ds(iface[f, q], 1)
-        work[where, :] = work[where, :] + stage[pl.ds(at + geo.off(q), 1), :]
-    primal = dot(inverse[f], work[...].astype(bf16))
-    low, high = limits(geo, lim, f)
-    return jnp.minimum(jnp.maximum(primal, low), high)
-
-
-def feeder_steps(geo, steps, iface, base, inverse, cost, target, thin, lim, recv,
-                 target_out, send, work, *stages):
-    chunk_in = recv.shape[0] // geo.D
-    chunk_out = steps * geo.X
-    arrived, leaving = stages[:steps], stages[steps:]
-    for s in range(steps):
-        unpack(geo, recv, arrived[s], chunk_in, s * geo.X)
-        leaving[s][...] = jnp.zeros_like(leaving[s])
-
-    def body(f, carry):
-        at = base[f]
-        c = cost[f]
-        work[...] = target[f]
-        for s in range(steps):
-            t = solve(geo, f, iface, base, inverse, cost, lim, work, arrived[s]) - c
-            if s < steps - 1:
-                work[...] = t
-            h = dot(thin[f], t.astype(bf16))
+        work[pl.ds(iface[q, f], 1), :] = rows[q]
+
+
+def feeder_pair(geo, last, iface, base, live, inverse, cost, rounded, kept, lim, recv, *rest):
+    if last:
+        result, send, inv, price, held, out, sems, out_sems = rest[:8]
+        rest = rest[8:]
+    else:
+        result, kept_out, send, inv, price, held, out, sems, out_sems = rest[:9]
+        rest = rest[9:]
+    ways = 1 if last else 2
+    arrived, leaving, works = rest[:2], rest[2 : 2 + ways], rest[2 + ways :]
+    side, bound, left, ahead = (works[i * GROUP : (i + 1) * GROUP] for i in range(4))
+    groups, load = moves(((inverse, inv), (cost, price), (rounded, held)), sems, GROUP)
+    _, store = moves(((out, result),), out_sems, GROUP)
+    for c in range(groups):
+        for i in range(3):
+            load(i, c).start()
+    for s in range(2):
+        unpack(geo, recv, arrived[s], 2 * geo.X, s * geo.X)
+    for stage in leaving:
+        stage[...] = jnp.zeros_like(stage)
+    if not last:
+        kept_out[...] = jnp.zeros_like(kept_out)
+
+    def body(c, carry):
+        for i in range(3):
+            load(i, c).wait()
+        fs = [c * GROUP + u for u in range(GROUP)]
+        for u, f in enumerate(fs):
+            side[u][...] = held[f].astype(f32)
+            rows = [kept[f, q : q + 1, :] for q in range(geo.Q)]
+            raise_rows(geo, f, iface, base, rows, side[u], arrived[0])
+        for u, f in enumerate(fs):
+            low, high = limits(geo, lim, f)
+            left[u][...] = clip(dot(inv[f], side[u][...].astype(bf16)), low, high) - price[f]
+        for u, f in enumerate(fs):
+            rows = [pick(left[u], iface, f, q) for q in range(geo.Q)]
+            raise_rows(geo, f, iface, base, rows, left[u], arrived[1])
+        for u, f in enumerate(fs):
+            low, high = limits(geo, lim, f)
+            primal = dot(inv[f], left[u][...].astype(bf16))
+            bound[u][...] = primal
+            anchor = clip(primal, low, high)
+            if last:
+                out[f] = anchor * jnp.where(f < live[0], 1.0, 0.0)
+            else:
+                t = anchor - price[f]
+                side[u][...] = t
+                t = t.astype(bf16)
+                out[f] = t
+                ahead[u][...] = dot(inv[f], t)
+        store(0, c).start()
+        for u, f in enumerate(fs):
+            at = base[f]
             for q in range(geo.Q):
-                leaving[s][pl.ds(at + geo.off(q), 1), :] = h[q : q + 1]
-        target_out[f] = t
+                leaving[0][pl.ds(at + geo.off(q), 1), :] = pick(bound[u], iface, f, q)
+                if not last:
+                    leaving[1][pl.ds(at + geo.off(q), 1), :] = pick(ahead[u], iface, f, q)
+                    kept_out[f, q : q + 1, :] = pick(side[u], iface, f, q)
         return carry
 
-    lax.fori_loop(0, geo.F, body, 0)
-    for s in range(steps):
-        pack(geo, leaving[s], send, chunk_out, s * geo.X)
-
-
-def feeder_last(geo, iface, base, live, inverse, cost, target, lim, recv, out, work, stage):
-    unpack(geo, recv, stage, recv.shape[0] // geo.D, geo.X)
-
-    def body(f, carry):
-        work[...] = target[f]
-        anchor = solve(geo, f, iface, base, inverse, cost, lim, work, stage)
-        out[f] = anchor * jnp.where(f < live[0], 1.0, 0.0)
-        return carry
-
-    lax.fori_loop(0, geo.F, body, 0)
+    lax.fori_loop(0, groups, body, 0)
+    for s in range(ways):
+        pack(geo, leaving[s], send, ways * geo.X, s * geo.X)
+    for c in range(groups):
+        store(0, c).wait()
 
 
 def slice_parity(geo, shape):
@@ -266,8 +327,8 @@
     inner = lane - (qps * RP + rps) * geo.L
     index = inner + slice_index * geo.L
     for q2 in range(Q2):
-        even = jnp.take_along_axis(aim[:, 2 * q2, :], index, axis=1)
-        odd = jnp.take_along_axis(aim[:, 2 * q2 + 1, :], index, axis=1)
+        even = jnp.take_along_axis(aim[2 * q2], index, axis=1)
+        odd = jnp.take_along_axis(aim[2 * q2 + 1], index, axis=1)
         scaled[:, q2 * LANES : (q2 + 1) * LANES] = w * jnp.where(qps == 0, even, odd)
     for par in range(2):
         for q2 in range(Q2):
@@ -380,7 +441,7 @@
 
 
 def owner_first(geo, slice_index, weight, aim, recv,
-                send, coef, hot_t, hot, act, scaled, den, count, dual, raised, old, norms):
+                send, coef, hot_t, hot, act, scaled, den, count, dual, old, norms):
     X = geo.X
     owner_setup(geo, slice_index[0], weight, aim, recv, coef, hot_t, hot, act, scaled, den, count)
     tables = (coef, hot_t, hot, act, scaled, den, count)
@@ -392,7 +453,6 @@
     u, v, z, p1, d1 = owner_step(geo, h, v, u, z, *tables)
     depart(geo, v, send, 2 * X, X)
     write_list(geo, dual, u)
-    write_list(geo, raised, v)
     write_list(geo, old, z)
     norms[...] = jnp.zeros_like(norms)
     for i, value in enumerate((p0, d0, p1, d1)):
@@ -400,30 +460,29 @@
 
 
 def owner_middle(geo, first, recv, coef, hot_t, hot, act, scaled, den, count,
-                 dual, raised, old, norms, send, dual_out, raised_out, old_out, norms_out):
+                 dual, old, norms, send, dual_out, old_out, norms_out):
     X = geo.X
     tables = (coef, hot_t, hot, act, scaled, den, count)
-    u, v, z = read_list(geo, dual), read_list(geo, raised), read_list(geo, old)
+    u, v, z = read_list(geo, dual), None, read_list(geo, old)
     norms_out[...] = norms[...]
     for s in range(2):
         h = arrive(geo, recv, 2 * X, s * X)
-        u, v, z, p, d = owner_step(geo, h, v, u, z, *tables)
+        u, v, z, p, d = owner_step(geo, h, v if s else None, u, z, *tables)
         depart(geo, v, send, 2 * X, s * X)
         at = 2 * (first + s)
         norms_out[at : at + 1] = p
         norms_out[at + 1 : at + 2] = d
     write_list(geo, dual_out, u)
-    write_list(geo, raised_out, v)
     write_list(geo, old_out, z)
 
 
 def owner_last(geo, recv, coef, hot_t, hot, act, scaled, den, count,
-               dual, raised, old, norms, send, agreed):
+               dual, old, norms, send, agreed):
     X, S, RP = geo.X, geo.S, geo.RP
     tables = (coef, hot_t, hot, act, scaled, den, count)
-    u, v, z = read_list(geo, dual), read_list(geo, raised), read_list(geo, old)
+    u, v, z = read_list(geo, dual), None, read_list(geo, old)
     h = arrive(geo, recv, X, 0)
-    u, v, z, p, d = owner_step(geo, h, v, u, z, *tables)
+    u, v, z, p, d = owner_step(geo, h, None, u, z, *tables)
     depart(geo, [PENALTY * x for x in u], send, X + 1, 0)
     at = 2 * (ITERS - 1)
     everything = norms[...]
@@ -450,7 +509,7 @@
     def body(f, carry):
         at = base[f]
         for q in range(geo.Q):
-            duals[f, q : q + 1, :] = stage[pl.ds(at + geo.off(q), 1), :]
+            duals[q, pl.ds(f, 1), :] = stage[pl.ds(at + geo.off(q), 1), :]
         return carry
 
     lax.fori_loop(0, geo.F, body, 0)
@@ -464,33 +523,87 @@
                 for j in range(G):
                     v = roll(sides[j], (j - (qp * RP + rp)) * L)
                     acc = v if acc is None else jnp.where(group_mask((part, LANES), j, L), v, acc)
-                consensus[rp * part : (rp + 1) * part, 2 * q2 + qp, :] = acc
+                consensus[2 * q2 + qp, rp * part : (rp + 1) * part, :] = acc
     line = jnp.sum(recv[pl.ds(X, geo.D, stride=X + 1), :], axis=0, keepdims=True)
-    line = jnp.sqrt(line)
+    line = jnp.broadcast_to(jnp.sqrt(line), (8, LANES))
+    side = iota((8, LANES), 0)
     lane = iota((8, LANES), 1)
-    wide = jnp.broadcast_to(line, (8, LANES))
     table = jnp.zeros((8, LANES), f32)
     for i in range(ITERS):
-        table = jnp.where(iota((8, LANES), 0) == i, roll(wide, -2 * i), table)
-    table = jnp.where(lane == 1, PENALTY * table, table)
-    norms[...] = table[:ITERS, :2]
+        table = jnp.where((lane == i) & (side == 0), roll(line, -i), table)
+        table = jnp.where((lane == i) & (side == 1), PENALTY * roll(line, -i - 1), table)
+    norms[...] = table[:2, :ITERS]
 
 
 VM = pltpu.VMEM
 SM = pltpu.SMEM
+HB = pltpu.HBM
 
 
 def call(body, args, ins, outs, scratch=(), name=None):
-    specs = [pl.BlockSpec(memory_space=s) for s in ins]
+    args = [
+        pltpu.with_memory_space_constraint(x, HB) if s is HB else x for x, s in zip(args, ins)
+    ]
     return pl.pallas_call(
         body,
-        in_specs=specs,
+        in_specs=[pl.BlockSpec(memory_space=s) for s in ins],
         out_specs=[pl.BlockSpec(memory_space=s) for _, _, s in outs],
-        out_shape=[jax.ShapeDtypeStruct(shape, dtype) for shape, dtype, _ in outs],
+        out_shape=[
+            jax.ShapeDtypeStruct(shape, dtype) if s is VM else s(shape, dtype)
+            for shape, dtype, s in outs
+        ],
         scratch_shapes=list(scratch),
         compiler_params=pltpu.CompilerParams(vmem_limit_bytes=40 << 20),
         name=name,
     )(*args)
+
+
+def feeder_calls(geo, iface, substation_of, live_count, inverse, cost, lower, upper):
+    F, K, C, D, X = geo.F, geo.K, geo.C, geo.D, geo.X
+    groups = F // GROUP
+    stage = pltpu.VMEM((geo.stage_rows, LANES), f32)
+    works = (pltpu.VMEM((K, LANES), f32),) * (4 * GROUP)
+    squares = pltpu.VMEM((F, K, K), bf16)
+    prices = pltpu.VMEM((F, K, C), f32)
+    halves = pltpu.VMEM((F, K, C), bf16)
+    carried = (((F, K, C), bf16, HB), ((F, 8, C), f32, VM))
+
+    def sems(count):
+        return pltpu.SemaphoreType.DMA((count, groups))
+
+    def begin():
+        rounded, kept, lim, base, send = call(
+            functools.partial(feeder_first, geo),
+            (iface, substation_of, live_count, inverse, cost, lower, upper),
+            (SM, SM, SM, HB, HB, VM, VM),
+            carried
+            + (
+                ((K, LANES), f32, VM),
+                ((F,), i32, SM),
+                ((D * (2 * X + 2), LANES), f32, VM),
+            ),
+            (squares, prices, halves, sems(2), sems(1),
+             stage, stage, pltpu.VMEM((2 * geo.NB, LANES), f32), pltpu.SMEM((geo.NB,), i32),
+             pltpu.SMEM((F,), i32)) + works,
+            "feeder_first",
+        )
+        return (rounded, kept, lim, base), base, send
+
+    def advance(state, recv, last):
+        rounded, kept, lim, base = state
+        out = call(
+            functools.partial(feeder_pair, geo, last),
+            (iface, base, live_count, inverse, cost, rounded, kept, lim, recv),
+            (SM, SM, SM, HB, HB, HB, VM, VM, VM),
+            ((((F, K, C), f32, HB),) if last else carried)
+            + (((D * (1 if last else 2) * X, LANES), f32, VM),),
+            (squares, prices, halves, prices if last else halves, sems(3), sems(1))
+            + (stage,) * (3 if last else 4) + works,
+            "feeder_last" if last else "feeder_pair",
+        )
+        return out if last else ((out[0], out[1], lim, base), out[2])
+
+    return begin, advance
 
 
 def shards(
@@ -517,34 +630,19 @@
         y = lax.all_to_all(y, ("sub", "fdr"), split_axis=0, concat_axis=0, tiled=True)
         return y.reshape(x.shape)
 
-    stage = pltpu.VMEM((geo.stage_rows, LANES), f32)
-    work = pltpu.VMEM((K, LANES), f32)
     slice_index = lax.axis_index("fdr").astype(i32).reshape(1)
-
-    target, thin, lim, base, send = call(
-        functools.partial(feeder_first, geo),
-        (iface_rows, substation_of, live_count, inverse, cost, lower_limit, upper_limit),
-        (SM, SM, SM, VM, VM, VM, VM),
-        (
-            ((F, K, C), f32, VM),
-            ((F, THIN, K), bf16, VM),
-            ((K, LANES), f32, VM),
-            ((F,), i32, SM),
-            ((D * (2 * X + 2), LANES), f32, VM),
-        ),
-        (stage, stage, pltpu.VMEM((2 * geo.NB, LANES), f32), pltpu.SMEM((geo.NB,), i32),
-         pltpu.SMEM((F,), i32)),
-        "feeder_first",
+    begin, advance = feeder_calls(
+        geo, iface_rows.T, substation_of, live_count, inverse, cost, lower_limit, upper_limit
     )
+    feeders, base, send = begin()
     state = (
-        ((n, wide), f32, VM),
         ((n, wide), f32, VM),
         ((S, wide), f32, VM),
         ((16, LANES), f32, VM),
     )
     out = call(
         functools.partial(owner_first, geo),
-        (slice_index, reserve_weight, reserve_target, swap(send)),
+        (slice_index, reserve_weight, jnp.swapaxes(reserve_target, 0, 1), swap(send)),
         (SM, SM, VM, VM),
         (
             ((D * 2 * X, LANES), f32, VM),
@@ -561,46 +659,23 @@
         "owner_first",
     )
     send, tables, memory = out[0], out[1:8], out[8:]
+
     for first in range(2, ITERS - 1, 2):
-        recv = swap(send)
-        target, send = call(
-            functools.partial(feeder_steps, geo, 2),
-            (iface_rows, base, inverse, cost, target, thin, lim, recv),
-            (SM, SM, VM, VM, VM, VM, VM, VM),
-            (((F, K, C), f32, VM), ((D * 2 * X, LANES), f32, VM)),
-            (work, stage, stage, stage, stage),
-            "feeder_steps",
-        )
+        feeders, send = advance(feeders, swap(send), False)
         out = call(
             functools.partial(owner_middle, geo, first),
             (swap(send), *tables, *memory),
-            (VM,) * 12,
+            (VM,) * 11,
             (((D * 2 * X, LANES), f32, VM),) + state,
             (),
             "owner_middle",
         )
         send, memory = out[0], out[1:]
-    recv = swap(send)
-    target, send = call(
-        functools.partial(feeder_steps, geo, 1),
-        (iface_rows, base, inverse, cost, target, thin, lim, recv),
-        (SM, SM, VM, VM, VM, VM, VM, VM),
-        (((F, K, C), f32, VM), ((D * X, LANES), f32, VM)),
-        (work, stage, stage),
-        "feeder_ahead",
-    )
-    (setpoints,) = call(
-        functools.partial(feeder_last, geo),
-        (iface_rows, base, live_count, inverse, cost, target, lim, recv),
-        (SM, SM, SM, VM, VM, VM, VM, VM),
-        (((F, K, C), f32, VM),),
-        (work, stage),
-        "feeder_last",
-    )
+    setpoints, send = advance(feeders, swap(send), True)
     send, agreed = call(
         functools.partial(owner_last, geo),
         (swap(send), *tables, *memory),
-        (VM,) * 12,
+        (VM,) * 11,
         (((D * (X + 1), LANES), f32, VM), ((Q2 * S // RP, LANES), f32, VM)),
         (),
         "owner_last",
@@ -610,11 +685,11 @@
         functools.partial(finish, geo),
         (base, swap(send), gathered),
         (SM, VM, VM),
-        (((F, Q, C), f32, VM), ((S, Q, C), f32, VM), ((ITERS, 2), f32, VM)),
-        (stage,),
+        (((Q, F, C), f32, VM), ((Q, S, C), f32, VM), ((2, ITERS), f32, VM)),
+        (pltpu.VMEM((geo.stage_rows, LANES), f32),),
         "finish",
     )
-    return duals, consensus, norms, setpoints
+    return jnp.swapaxes(duals, 0, 1), jnp.swapaxes(consensus, 0, 1), norms.T, setpoints
 
 
 def solution(mesh):

time: 177 us -> 122 us (0.69)
  Pallas kernels: 70.1 us -> 35.5 us
  local copies, waits for them, and re-layouts: 26.3 us -> 2.86 us
  waiting for transfers between devices: 12 us -> 15.1 us
    pallas_call x8 -> x7, Pallas kernels: 70.1 us -> 35.5 us  [call(): pl.pallas_call(body, in_specs=[pl.BlockSpec(memory_space=s) for s in ins]...]
    unnamed x37 -> x14, local copies, waits for them, and re-layouts: 26.3 us -> 2.86 us
    all_to_all x2, waiting for transfers between devices: 12 us -> 15.1 us  [swap(): lax.all_to_all(y, ('sub', 'fdr'), split_axis=0, concat_axis=0, tiled=True)]
  transfers between devices with their start and end apart: 2 -> 2, of which waited for: 1 -> 2; matrix products, arithmetic and copies ran while one was open for 0% -> 0% of each run, Pallas kernels for 6% -> 0%
where the time goes in v2:
time: 122 us; the launch traced here: 121 us
  blocking collectives  56.6 us (46%)
  Pallas kernels  35.5 us (29%)
  waiting for transfers between devices  15.1 us (12%)
  starting transfers between devices  9.91 us (8%)
  local copies, waits for them, and re-layouts  2.86 us (2%)
  between operations  1.35 us (1%)
    all_to_all x4, blocking collectives, swap(): lax.all_to_all(y, ('sub', 'fdr'), split_axis=0, concat_axis=0, tiled=True)  51 us
    pallas_call x7, Pallas kernels, call(): pl.pallas_call(body, in_specs=[pl.BlockSpec(memory_space=s) for s in ins]...  35.5 us
    all_to_all x2, waiting for transfers between devices, swap(): lax.all_to_all(y, ('sub', 'fdr'), split_axis=0, concat_axis=0, tiled=True)  15.1 us
    all_to_all x2, starting transfers between devices, swap(): lax.all_to_all(y, ('sub', 'fdr'), split_axis=0, concat_axis=0, tiled=True)  9.91 us
    all_gather x1, blocking collectives, shards(): gathered = lax.all_gather(agreed, 'fdr', axis=0, tiled=True)  5.55 us
    unnamed x14, local copies, waits for them, and re-layouts  2.86 us
  transfers between devices with their start and end apart: 2, of which 2 were waited for; matrix products, arithmetic and copies ran while one was open for 0% of the time, Pallas kernels for 0%

profile of v2, /device:TPU:0, one launch (start us, length us, event | category | flops | bytes accessed | tf_op | source)
XLA Modules:
  0.0 121.4 jit_solution(2603833593483792966)
XLA Ops:
  1.3 0.0 copy-start.1
  1.3 0.7 copy-done.1
  2.0 0.0 copy-start.3
  2.0 0.8 copy-done.3
  2.7 0.0 copy-start.4
  2.7 0.8 copy-done.4
  3.5 0.0 copy-start.5
  3.5 0.7 copy-done.5
  4.1 0.0 copy-start
  4.1 0.0 copy-start.6
  4.1 0.0 copy-start.2
  4.1 9.8 %feeder_first.1 = (bf16[32,256,128]{2,1,0:T(8,128)(2,1)}, f32[32,8,128]{2,1,0:T(8,128)S(1)}, f32[256,128]{1,0:T(8,128)S(1)}, s32[32]{0:T(128)S(4)}, f32[640,128]{1,0:T(8,128)}) custom-call(s32[6,32]{1,0:T(8,128)S(1)} %bitcast.29, s32[32]{0:T(128)S(1)} %copy-done.5, s32[1]{0:T(128)S(6)} %copy.19.live, bf16[32,256,256]{2,1,0:T(8,128)(2,1)} %inverse.5, ...), custom_call_target="tpu_custom_call" | custom-call | tf_op jit(solution)/shard_map/feeder_first/pallas_call | solution.py:547
  13.9 7.3 %all-to-all-start = ((f32[32,1,2560]{2,1,0:T(1,128)}), f32[32,1,2560]{2,1,0:T(1,128)S(1)}, u32[]{:S(2)}, u32[]{:S(2)}) async-start(f32[32,1,2560]{2,1,0:T(1,128)} %bitcast.3), calls=%async_computation | async-start | bytes 655360 | tf_op jit(solution)/shard_map/all_to_all | solution.py:630
  21.3 12.0 %all-to-all-done = f32[32,1,2560]{2,1,0:T(1,128)S(1)} async-done(((f32[32,1,2560]{2,1,0:T(1,128)}), f32[32,1,2560]{2,1,0:T(1,128)S(1)}, u32[]{:S(2)}, u32[]{:S(2)}) %all-to-all-start) | async-done | bytes 327712 | tf_op jit(solution)/shard_map/all_to_all | solution.py:630
  33.3 0.0 copy-done
  33.3 0.0 copy-done.6
  33.3 2.0 %owner_first.1 = (f32[576,128]{1,0:T(8,128)S(1)}, f32[18,96,128]{2,1,0:T(8,128)S(1)}, bf16[3,64,32]{2,1,0:T(8,128)(2,1)S(1)}, bf16[192,32]{1,0:T(8,128)(2,1)S(1)...) custom-call(s32[1]{0:T(128)} %bitcast.1.slice_index, ...), custom_call_target="tpu_custom_call" | custom-call | tf_op jit(solution)/shard_map/owner_first/pallas_call | solution.py:547
  35.4 13.5 %all_to_all.30 = f32[32,1,2304]{2,1,0:T(1,128)S(1)} all-to-all(f32[32,1,2304]{2,1,0:T(1,128)S(1)} %bitcast.24), channel_id=1, replica_groups=mesh['sub'=8,'fdr'=4] {'sub','fdr'}, dimensions={0} | all-to-all | bytes 589824 | tf_op jit(solution)/shard_map/all_to_all | solution.py:630
  48.9 0.0 copy-done.2
  48.9 11.2 %feeder_pair.1 = (bf16[32,256,128]{2,1,0:T(8,128)(2,1)}, f32[32,8,128]{2,1,0:T(8,128)S(1)}, f32[576,128]{1,0:T(8,128)S(1)}) custom-call(s32[6,32]{1,0:T(8,128)S(1)} %bitcast.30, s32[32]{0:T(128)S(4)} %get-tuple-element.34.base, s32[1]{0:T(128)S(6)} %copy.19.live, bf16[32,256,256]{2,1,0:T(8,128)(2,1)} %inverse.5, f32[32,256,128]{2,1,0:T(8,128)} %cost.5, ...), custom_call_target="tpu_custom_call" | custom-call | tf_op jit(solution)/shard_map/feeder_pair/pallas_call | solution.py:547
  60.1 13.5 %all_to_all.31 = f32[32,1,2304]{2,1,0:T(1,128)S(1)} all-to-all(f32[32,1,2304]{2,1,0:T(1,128)S(1)} %bitcast.26), channel_id=1, replica_groups=mesh['sub'=8,'fdr'=4] {'sub','fdr'}, dimensions={0} | all-to-all | bytes 589824 | tf_op jit(solution)/shard_map/all_to_all | solution.py:630
  73.6 1.2 owner_middle.1
  74.8 13.5 %all_to_all.32 = f32[32,1,2304]{2,1,0:T(1,128)S(1)} all-to-all(f32[32,1,2304]{2,1,0:T(1,128)S(1)} %bitcast.25), channel_id=1, replica_groups=mesh['sub'=8,'fdr'=4] {'sub','fdr'}, dimensions={0} | all-to-all | bytes 589824 | tf_op jit(solution)/shard_map/all_to_all | solution.py:630
  88.3 8.8 %feeder_last.1 = (f32[32,256,128]{2,1,0:T(8,128)}, f32[288,128]{1,0:T(8,128)S(1)}) custom-call(s32[6,32]{1,0:T(8,128)S(1)} %bitcast.31, s32[32]{0:T(128)S(4)} %get-tuple-element.34.base, s32[1]{0:T(128)S(6)} %copy.19.live, bf16[32,256,256]{2,1,0:T(8,128)(2,1)} %inverse.5, f32[32,256,128]{2,1,0:T(8,128)} %cost.5, ...), custom_call_target="tpu_custom_call" | custom-call | tf_op jit(solution)/shard_map/feeder_last/pallas_call | solution.py:547
  97.1 10.5 %all_to_all.33 = f32[32,1,1152]{2,1,0:T(1,128)S(1)} all-to-all(f32[32,1,1152]{2,1,0:T(1,128)S(1)} %bitcast.27), channel_id=1, replica_groups=mesh['sub'=8,'fdr'=4] {'sub','fdr'}, dimensions={0} | all-to-all | bytes 294912 | tf_op jit(solution)/shard_map/all_to_all | solution.py:630
  107.6 1.3 %owner_last.1 = (f32[320,128]{1,0:T(8,128)}, f32[48,128]{1,0:T(8,128)S(1)}) custom-call(f32[288,128]{1,0:T(8,128)S(1)} %bitcast.23, f32[18,96,128]{2,1,0:T(8,128)S(1)} %get-tuple-element.43.coef, bf16[3,64,32]{2,1,0:T(8,128)(2,1)S(1)} %get-tuple-element.44.hot_t, bf16[192,32]{1,0:T(8,128)(2,1)S(1)} %get-tuple-element.45.hot, ...), custom_call_target="tpu_custom_call" | custom-call | tf_op jit(solution)/shard_map/owner_last/pallas_call | solution.py:547
  109.0 2.6 %all-to-all-start.5 = ((f32[32,1,1280]{2,1,0:T(1,128)}), f32[32,1,1280]{2,1,0:T(1,128)S(1)}, u32[]{:S(2)}, u32[]{:S(2)}) async-start(f32[32,1,1280]{2,1,0:T(1,128)} %bitcast.13), calls=%async_computation.5 | async-start | bytes 327680 | tf_op jit(solution)/shard_map/all_to_all | solution.py:630
  111.6 5.5 %all_gather.3.agreed = f32[192,128]{1,0:T(8,128)S(1)} all-gather(f32[48,128]{1,0:T(8,128)S(1)} %get-tuple-element.59), channel_id=1, replica_groups=mesh['sub'=8,'fdr'=4] {'fdr'}, dimensions={0}, use_global_device_ids=true | all-gather | bytes 122880 | tf_op jit(solution)/shard_map/all_gather | solution.py:683
  117.1 3.1 %all-to-all-done.5 = f32[32,1,1280]{2,1,0:T(1,128)S(1)} async-done(((f32[32,1,1280]{2,1,0:T(1,128)}), f32[32,1,1280]{2,1,0:T(1,128)S(1)}, u32[]{:S(2)}, u32[]{:S(2)}) %all-to-all-start.5) | async-done | bytes 163872 | tf_op jit(solution)/shard_map/all_to_all | solution.py:630
  120.2 1.2 finish.1
Async XLA Ops:
  1.3 0.7 copy-start.1
  2.0 0.8 copy-start.3
  2.7 0.8 copy-start.4
  3.5 0.7 copy-start.5
  4.1 29.2 %copy-start = (f32[32,6,128]{2,0,1:T(8,128)S(1)}, f32[32,6,128]{2,0,1:T(8,128)}, u32[]{:S(2)}) copy-start(f32[32,6,128]{2,0,1:T(8,128)} %param.17) | copy-start | bytes 294916
  4.1 29.2 %copy-start.6 = (f32[32]{0:T(128)S(1)}, f32[32]{0:T(128)}, u32[]{:S(2)}) copy-start(f32[32]{0:T(128)} %weight.1) | copy-start | bytes 388
  4.1 44.8 %copy-start.2 = (s32[32,6]{0,1:T(8,128)S(1)}, s32[32,6]{0,1:T(8,128)}, u32[]{:S(2)}) copy-start(s32[32,6]{0,1:T(8,128)} %param.13) | copy-start | bytes 2308
  13.9 19.4 %all-to-all-start = ((f32[32,1,2560]{2,1,0:T(1,128)}), f32[32,1,2560]{2,1,0:T(1,128)S(1)}, u32[]{:S(2)}, u32[]{:S(2)}) async-start(f32[32,1,2560]{2,1,0:T(1,128)} %bitcast.3), calls=%async_computation | async-start | bytes 655360 | tf_op jit(solution)/shard_map/all_to_all | solution.py:630
  109.0 11.2 %all-to-all-start.5 = ((f32[32,1,1280]{2,1,0:T(1,128)}), f32[32,1,1280]{2,1,0:T(1,128)S(1)}, u32[]{:S(2)}, u32[]{:S(2)}) async-start(f32[32,1,1280]{2,1,0:T(1,128)} %bitcast.13), calls=%async_computation.5 | async-start | bytes 327680 | tf_op jit(solution)/shard_map/all_to_all | solution.py:630

commit v3 on v2

--- a/solution.py
+++ b/solution.py
@@ -11,7 +11,8 @@
 PENALTY = 2.0
 LANES = 128
 THIN = 16
-GROUP = 4
+GROUP = 8
+PIECE = 4
 
 f32 = jnp.float32
 bf16 = jnp.bfloat16
@@ -90,26 +91,34 @@
     return jnp.dot(a, b, preferred_element_type=f32)
 
 
-def limits(geo, lim, f):
-    table = lim[...]
-    low = jnp.take_along_axis(table, jnp.full((geo.K, LANES), f, i32), axis=1)
-    high = jnp.take_along_axis(table, jnp.full((geo.K, LANES), f + geo.F, i32), axis=1)
-    return low, high
+def limits(geo, turned, u):
+    shape = (geo.K, LANES)
+    low = jnp.broadcast_to(turned[:, u : u + 1], shape)
+    return low, jnp.broadcast_to(turned[:, geo.F + u : geo.F + u + 1], shape)
 
 
 def clip(x, low, high):
     return jnp.minimum(jnp.maximum(x, low), high)
 
 
-def moves(pairs, sems, group):
-    count = pairs[0][0].shape[0] // group
-
+def moves(pairs, sems, size):
     def one(i, c):
         src, dst = pairs[i]
-        part = pl.ds(c * group, group)
+        part = pl.ds(c * size, size)
         return pltpu.make_async_copy(src.at[part], dst.at[part], sems.at[i, c])
 
-    return count, one
+    return pairs[0][0].shape[0] // size, one
+
+
+def sweep(slots, body):
+    body(0, PIECE)
+    body(PIECE, PIECE)
+
+    def step(i, carry):
+        body((i + 1) * GROUP, GROUP)
+        return carry
+
+    lax.fori_loop(0, slots // GROUP - 1, step, 0)
 
 
 def pick(work, iface, f, q):
@@ -119,13 +128,19 @@
 def feeder_first(geo, iface, sub, live, inverse, cost, lower, upper,
                  rounded, kept, lim, base, send,
                  inv, price, out, sems, out_sems,
-                 stage1, stage2, meta, count, rank, *works):
+                 stage1, stage2, meta, count, rank, edge, edge_sems, turned, *works):
     F, K, Q, NB, X = geo.F, geo.K, geo.Q, geo.NB, geo.X
     chunk = 2 * X + 2
     bound, square, left, ahead = (works[i * GROUP : (i + 1) * GROUP] for i in range(4))
-    groups, load = moves(((inverse, inv), (cost, price)), sems, GROUP)
-    _, store = moves(((out, rounded),), out_sems, GROUP)
-    for c in range(groups):
+    pieces, load = moves(((inverse, inv), (cost, price)), sems, PIECE)
+    _, store = moves(((out, rounded),), out_sems, PIECE)
+    sides = [
+        pltpu.make_async_copy(x, edge.at[pl.ds(i * F, F)], edge_sems.at[i])
+        for i, x in enumerate((lower, upper))
+    ]
+    for copy in sides:
+        copy.start()
+    for c in range(pieces):
         for i in range(2):
             load(i, c).start()
     for k in range(NB):
@@ -140,10 +155,10 @@
         return carry
 
     lax.fori_loop(0, F, place, 0)
-    stacked = jnp.concatenate(
-        [lower[...], upper[...], jnp.zeros((LANES - 2 * F, K), f32)], axis=0
-    )
-    lim[...] = stacked.T
+    edge[2 * F :, :] = jnp.zeros((LANES - 2 * F, K), f32)
+    for copy in sides:
+        copy.wait()
+    lim[...] = edge[...].T
     stage1[...] = jnp.zeros_like(stage1)
     stage2[...] = jnp.zeros_like(stage2)
     meta[...] = jnp.zeros_like(meta)
@@ -154,46 +169,48 @@
         third = third + jnp.where(lane >= i * geo.PR * Q, 1, 0)
     within = lane - third * (geo.PR * Q)
 
-    def body(c, carry):
-        for i in range(2):
-            load(i, c).wait()
-        fs = [c * GROUP + u for u in range(GROUP)]
+    def body(at, size):
+        for c in range(size // PIECE):
+            for i in range(2):
+                load(i, at // PIECE + c).wait()
+        fs = [at + u for u in range(size)]
+        turned[...] = pltpu.roll(lim[...], LANES - at, 1)
         for u, f in enumerate(fs):
-            at = within - rank[f] * Q
+            near = within - rank[f] * Q
             chosen = jnp.full((1, LANES), -1, i32)
             for q in range(Q):
-                chosen = jnp.where((at == q) & (third < geo.Q2), iface[q, f], chosen)
+                chosen = jnp.where((near == q) & (third < geo.Q2), iface[q, f], chosen)
             hot = (iota((K, LANES), 0) == jnp.broadcast_to(chosen, (K, LANES))).astype(f32)
             price_u = price[f]
             both = dot(inv[f], jnp.concatenate([-price_u, hot], axis=1).astype(bf16))
             primal = both[:, :LANES]
             bound[u][...] = primal
             square[u][...] = both[:, LANES:]
-            low, high = limits(geo, lim, f)
+            low, high = limits(geo, turned, u)
             t = clip(primal, low, high) - price_u
             left[u][...] = t
             t = t.astype(bf16)
             out[f] = t
             ahead[u][...] = dot(inv[f], t)
-        store(0, c).start()
+            if u % PIECE == PIECE - 1:
+                store(0, at // PIECE + u // PIECE).start()
         for u, f in enumerate(fs):
             k = lax.div(sub[f], geo.S)
             ident = jnp.where(f < live[0], sub[f] - k * geo.S + 1, 0).astype(f32)
             lines = [jnp.where(lane == geo.id_lane + rank[f], ident, 0.0),
                      jnp.zeros((1, LANES), f32)]
-            at = base[f]
+            to = base[f]
             for q in range(Q):
                 m, i = divmod(q, geo.Q2)
                 lines[m] = lines[m] + jnp.where(third == i, pick(square[u], iface, f, q), 0.0)
-                stage1[pl.ds(at + geo.off(q), 1), :] = pick(bound[u], iface, f, q)
-                stage2[pl.ds(at + geo.off(q), 1), :] = pick(ahead[u], iface, f, q)
+                stage1[pl.ds(to + geo.off(q), 1), :] = pick(bound[u], iface, f, q)
+                stage2[pl.ds(to + geo.off(q), 1), :] = pick(ahead[u], iface, f, q)
                 kept[f, q : q + 1, :] = pick(left[u], iface, f, q)
             for m in range(2):
                 spot = pl.ds(m * NB + k, 1)
                 meta[spot, :] = meta[spot, :] + lines[m]
-        return carry
-
-    lax.fori_loop(0, groups, body, 0)
+
+    sweep(F, body)
     pack(geo, stage1, send, chunk, 0)
     pack(geo, stage2, send, chunk, X)
     for j in range(geo.G):
@@ -201,7 +218,7 @@
             send[pl.ds(j * chunk + 2 * X + m, NB, stride=geo.G * chunk), :] = meta[
                 m * NB : (m + 1) * NB
             ]
-    for c in range(groups):
+    for c in range(pieces):
         store(0, c).wait()
 
 
@@ -221,10 +238,11 @@
         rest = rest[9:]
     ways = 1 if last else 2
     arrived, leaving, works = rest[:2], rest[2 : 2 + ways], rest[2 + ways :]
-    side, bound, left, ahead = (works[i * GROUP : (i + 1) * GROUP] for i in range(4))
-    groups, load = moves(((inverse, inv), (cost, price), (rounded, held)), sems, GROUP)
-    _, store = moves(((out, result),), out_sems, GROUP)
-    for c in range(groups):
+    turned, works = works[0], works[1:]
+    side, bound, left, ahead, lows, highs = (works[i * GROUP : (i + 1) * GROUP] for i in range(6))
+    pieces, load = moves(((inverse, inv), (cost, price), (rounded, held)), sems, PIECE)
+    _, store = moves(((out, result),), out_sems, PIECE)
+    for c in range(pieces):
         for i in range(3):
             load(i, c).start()
     for s in range(2):
@@ -234,22 +252,26 @@
     if not last:
         kept_out[...] = jnp.zeros_like(kept_out)
 
-    def body(c, carry):
-        for i in range(3):
-            load(i, c).wait()
-        fs = [c * GROUP + u for u in range(GROUP)]
+    def body(at, size):
+        for c in range(size // PIECE):
+            for i in range(3):
+                load(i, at // PIECE + c).wait()
+        fs = [at + u for u in range(size)]
+        turned[...] = pltpu.roll(lim[...], LANES - at, 1)
         for u, f in enumerate(fs):
             side[u][...] = held[f].astype(f32)
             rows = [kept[f, q : q + 1, :] for q in range(geo.Q)]
             raise_rows(geo, f, iface, base, rows, side[u], arrived[0])
         for u, f in enumerate(fs):
-            low, high = limits(geo, lim, f)
+            low, high = limits(geo, turned, u)
+            lows[u][...] = low
+            highs[u][...] = high
             left[u][...] = clip(dot(inv[f], side[u][...].astype(bf16)), low, high) - price[f]
         for u, f in enumerate(fs):
             rows = [pick(left[u], iface, f, q) for q in range(geo.Q)]
             raise_rows(geo, f, iface, base, rows, left[u], arrived[1])
         for u, f in enumerate(fs):
-            low, high = limits(geo, lim, f)
+            low, high = lows[u][...], highs[u][...]
             primal = dot(inv[f], left[u][...].astype(bf16))
             bound[u][...] = primal
             anchor = clip(primal, low, high)
@@ -261,20 +283,20 @@
                 t = t.astype(bf16)
                 out[f] = t
                 ahead[u][...] = dot(inv[f], t)
-        store(0, c).start()
+            if u % PIECE == PIECE - 1:
+                store(0, at // PIECE + u // PIECE).start()
         for u, f in enumerate(fs):
-            at = base[f]
+            to = base[f]
             for q in range(geo.Q):
-                leaving[0][pl.ds(at + geo.off(q), 1), :] = pick(bound[u], iface, f, q)
+                leaving[0][pl.ds(to + geo.off(q), 1), :] = pick(bound[u], iface, f, q)
                 if not last:
-                    leaving[1][pl.ds(at + geo.off(q), 1), :] = pick(ahead[u], iface, f, q)
+                    leaving[1][pl.ds(to + geo.off(q), 1), :] = pick(ahead[u], iface, f, q)
                     kept_out[f, q : q + 1, :] = pick(side[u], iface, f, q)
-        return carry
-
-    lax.fori_loop(0, groups, body, 0)
+
+    sweep(geo.F, body)
     for s in range(ways):
         pack(geo, leaving[s], send, ways * geo.X, s * geo.X)
-    for c in range(groups):
+    for c in range(pieces):
         store(0, c).wait()
 
 
@@ -538,12 +560,15 @@
 VM = pltpu.VMEM
 SM = pltpu.SMEM
 HB = pltpu.HBM
+SMH = 0
 
 
 def call(body, args, ins, outs, scratch=(), name=None):
     args = [
-        pltpu.with_memory_space_constraint(x, HB) if s is HB else x for x, s in zip(args, ins)
+        pltpu.with_memory_space_constraint(x, HB) if s in (HB, SMH) else x
+        for x, s in zip(args, ins)
     ]
+    ins = [SM if s is SMH else s for s in ins]
     return pl.pallas_call(
         body,
         in_specs=[pl.BlockSpec(memory_space=s) for s in ins],
@@ -560,7 +585,7 @@
 
 def feeder_calls(geo, iface, substation_of, live_count, inverse, cost, lower, upper):
     F, K, C, D, X = geo.F, geo.K, geo.C, geo.D, geo.X
-    groups = F // GROUP
+    pieces = F // PIECE
     stage = pltpu.VMEM((geo.stage_rows, LANES), f32)
     works = (pltpu.VMEM((K, LANES), f32),) * (4 * GROUP)
     squares = pltpu.VMEM((F, K, K), bf16)
@@ -569,13 +594,13 @@
     carried = (((F, K, C), bf16, HB), ((F, 8, C), f32, VM))
 
     def sems(count):
-        return pltpu.SemaphoreType.DMA((count, groups))
+        return pltpu.SemaphoreType.DMA((count, pieces))
 
     def begin():
         rounded, kept, lim, base, send = call(
             functools.partial(feeder_first, geo),
             (iface, substation_of, live_count, inverse, cost, lower, upper),
-            (SM, SM, SM, HB, HB, VM, VM),
+            (SMH, SMH, SM, HB, HB, HB, HB),
             carried
             + (
                 ((K, LANES), f32, VM),
@@ -584,7 +609,8 @@
             ),
             (squares, prices, halves, sems(2), sems(1),
              stage, stage, pltpu.VMEM((2 * geo.NB, LANES), f32), pltpu.SMEM((geo.NB,), i32),
-             pltpu.SMEM((F,), i32)) + works,
+             pltpu.SMEM((F,), i32), pltpu.VMEM((LANES, K), f32),
+             pltpu.SemaphoreType.DMA((2,)), pltpu.VMEM((K, LANES), f32)) + works,
             "feeder_first",
         )
         return (rounded, kept, lim, base), base, send
@@ -598,7 +624,7 @@
             ((((F, K, C), f32, HB),) if last else carried)
             + (((D * (1 if last else 2) * X, LANES), f32, VM),),
             (squares, prices, halves, prices if last else halves, sems(3), sems(1))
-            + (stage,) * (3 if last else 4) + works,
+            + (stage,) * (3 if last else 4) + (pltpu.VMEM((K, LANES), f32),) + works + works[: 2 * GROUP],
             "feeder_last" if last else "feeder_pair",
         )
         return out if last else ((out[0], out[1], lim, base), out[2])

time: 122 us -> 115 us (0.943)
  Pallas kernels: 35.5 us -> 32 us
  local copies, waits for them, and re-layouts: 2.86 us -> 0.01 us
    pallas_call x7, Pallas kernels: 35.5 us -> 32 us  [call(): pl.pallas_call(body, in_specs=[pl.BlockSpec(memory_space=s) for s in ins]...]
    unnamed x14 -> x6, local copies, waits for them, and re-layouts: 2.86 us -> 0.01 us
where the time goes in v3:
time: 115 us
  blocking collectives  56.5 us (49%)
  Pallas kernels  32 us (28%)
  waiting for transfers between devices  15.1 us (13%)
  starting transfers between devices  9.89 us (9%)
  between operations  1.36 us (1%)
    all_to_all x4, blocking collectives, swap(): lax.all_to_all(y, ('sub', 'fdr'), split_axis=0, concat_axis=0, tiled=True)  51 us
    pallas_call x7, Pallas kernels, call(): pl.pallas_call(body, in_specs=[pl.BlockSpec(memory_space=s) for s in ins]...  32 us
    all_to_all x2, waiting for transfers between devices, swap(): lax.all_to_all(y, ('sub', 'fdr'), split_axis=0, concat_axis=0, tiled=True)  15.1 us
    all_to_all x2, starting transfers between devices, swap(): lax.all_to_all(y, ('sub', 'fdr'), split_axis=0, concat_axis=0, tiled=True)  9.89 us
    all_gather x1, blocking collectives, shards(): gathered = lax.all_gather(agreed, 'fdr', axis=0, tiled=True)  5.55 us
  transfers between devices with their start and end apart: 2, of which 2 were waited for; matrix products, arithmetic and copies ran while one was open for 0% of the time, Pallas kernels for 0%

profile of v3, /device:TPU:0, one launch (start us, length us, event | category | flops | bytes accessed | tf_op | source)
XLA Modules:
  0.0 114.9 jit_solution(11872591013185857363)
XLA Ops:
  1.3 0.0 copy-start
  1.3 0.0 copy-start.2
  1.3 0.0 copy-start.1
  1.3 10.5 %feeder_first.1 = (bf16[32,256,128]{2,1,0:T(8,128)(2,1)}, f32[32,8,128]{2,1,0:T(8,128)S(1)}, f32[256,128]{1,0:T(8,128)S(1)}, s32[32]{0:T(128)S(4)}, f32[640,128]{1,0:T(8,128)}) custom-call(s32[6,32]{1,0:T(8,128)} %bitcast.29, s32[32]{0:T(128)} %sub.1, s32[1]{0:T(128)S(6)} %copy.19.live, bf16[32,256,256]{2,1,0:T(8,128)(2,1)} %inverse.5, ...), custom_call_target="tpu_custom_call" | custom-call | tf_op jit(solution)/shard_map/feeder_first/pallas_call | solution.py:572
  11.8 7.3 %all-to-all-start = ((f32[32,1,2560]{2,1,0:T(1,128)}), f32[32,1,2560]{2,1,0:T(1,128)S(1)}, u32[]{:S(2)}, u32[]{:S(2)}) async-start(f32[32,1,2560]{2,1,0:T(1,128)} %bitcast.3), calls=%async_computation | async-start | bytes 655360 | tf_op jit(solution)/shard_map/all_to_all | solution.py:656
  19.1 12.0 %all-to-all-done = f32[32,1,2560]{2,1,0:T(1,128)S(1)} async-done(((f32[32,1,2560]{2,1,0:T(1,128)}), f32[32,1,2560]{2,1,0:T(1,128)S(1)}, u32[]{:S(2)}, u32[]{:S(2)}) %all-to-all-start) | async-done | bytes 327712 | tf_op jit(solution)/shard_map/all_to_all | solution.py:656
  31.1 0.0 copy-done
  31.1 0.0 copy-done.2
  31.1 2.0 %owner_first.1 = (f32[576,128]{1,0:T(8,128)S(1)}, f32[18,96,128]{2,1,0:T(8,128)S(1)}, bf16[3,64,32]{2,1,0:T(8,128)(2,1)S(1)}, bf16[192,32]{1,0:T(8,128)(2,1)S(1)...) custom-call(s32[1]{0:T(128)} %bitcast.1.slice_index, ...), custom_call_target="tpu_custom_call" | custom-call | tf_op jit(solution)/shard_map/owner_first/pallas_call | solution.py:572
  33.2 13.5 %all_to_all.30 = f32[32,1,2304]{2,1,0:T(1,128)S(1)} all-to-all(f32[32,1,2304]{2,1,0:T(1,128)S(1)} %bitcast.24), channel_id=1, replica_groups=mesh['sub'=8,'fdr'=4] {'sub','fdr'}, dimensions={0} | all-to-all | bytes 589824 | tf_op jit(solution)/shard_map/all_to_all | solution.py:656
  46.7 0.0 copy-done.1
  46.7 8.3 %feeder_pair.1 = (bf16[32,256,128]{2,1,0:T(8,128)(2,1)}, f32[32,8,128]{2,1,0:T(8,128)S(1)}, f32[576,128]{1,0:T(8,128)S(1)}) custom-call(s32[6,32]{1,0:T(8,128)S(1)} %bitcast.30, s32[32]{0:T(128)S(4)} %get-tuple-element.34.base, s32[1]{0:T(128)S(6)} %copy.19.live, bf16[32,256,256]{2,1,0:T(8,128)(2,1)} %inverse.5, f32[32,256,128]{2,1,0:T(8,128)} %cost.5, ...), custom_call_target="tpu_custom_call" | custom-call | tf_op jit(solution)/shard_map/feeder_pair/pallas_call | solution.py:572
  55.1 13.5 %all_to_all.31 = f32[32,1,2304]{2,1,0:T(1,128)S(1)} all-to-all(f32[32,1,2304]{2,1,0:T(1,128)S(1)} %bitcast.26), channel_id=1, replica_groups=mesh['sub'=8,'fdr'=4] {'sub','fdr'}, dimensions={0} | all-to-all | bytes 589824 | tf_op jit(solution)/shard_map/all_to_all | solution.py:656
  68.5 1.2 %owner_middle.1 = (f32[576,128]{1,0:T(8,128)S(1)}, f32[96,384]{1,0:T(8,128)S(1)}, f32[32,384]{1,0:T(8,128)S(1)}, f32[16,128]{1,0:T(8,128)S(1)}) custom-call(f32[576,128]{1,0:T(8,128)S(1)} %bitcast.19, f32[18,96,128]{2,1,0:T(8,128)S(1)} %get-tuple-element.43.coef, bf16[3,64,32]{2,1,0:T(8,128)(2,1)S(1)} %get-tuple-element.44.hot_t, ...), custom_call_target="tpu_custom_call" | custom-call | tf_op jit(solution)/shard_map/owner_middle/pallas_call | solution.py:572
  69.8 13.5 %all_to_all.32 = f32[32,1,2304]{2,1,0:T(1,128)S(1)} all-to-all(f32[32,1,2304]{2,1,0:T(1,128)S(1)} %bitcast.25), channel_id=1, replica_groups=mesh['sub'=8,'fdr'=4] {'sub','fdr'}, dimensions={0} | all-to-all | bytes 589824 | tf_op jit(solution)/shard_map/all_to_all | solution.py:656
  83.2 7.4 %feeder_last.1 = (f32[32,256,128]{2,1,0:T(8,128)}, f32[288,128]{1,0:T(8,128)S(1)}) custom-call(s32[6,32]{1,0:T(8,128)S(1)} %bitcast.31, s32[32]{0:T(128)S(4)} %get-tuple-element.34.base, s32[1]{0:T(128)S(6)} %copy.19.live, bf16[32,256,256]{2,1,0:T(8,128)(2,1)} %inverse.5, f32[32,256,128]{2,1,0:T(8,128)} %cost.5, ...), custom_call_target="tpu_custom_call" | custom-call | tf_op jit(solution)/shard_map/feeder_last/pallas_call | solution.py:572
  90.7 10.5 %all_to_all.33 = f32[32,1,1152]{2,1,0:T(1,128)S(1)} all-to-all(f32[32,1,1152]{2,1,0:T(1,128)S(1)} %bitcast.27), channel_id=1, replica_groups=mesh['sub'=8,'fdr'=4] {'sub','fdr'}, dimensions={0} | all-to-all | bytes 294912 | tf_op jit(solution)/shard_map/all_to_all | solution.py:656
  101.2 1.3 %owner_last.1 = (f32[320,128]{1,0:T(8,128)}, f32[48,128]{1,0:T(8,128)S(1)}) custom-call(f32[288,128]{1,0:T(8,128)S(1)} %bitcast.23, f32[18,96,128]{2,1,0:T(8,128)S(1)} %get-tuple-element.43.coef, bf16[3,64,32]{2,1,0:T(8,128)(2,1)S(1)} %get-tuple-element.44.hot_t, bf16[192,32]{1,0:T(8,128)(2,1)S(1)} %get-tuple-element.45.hot, ...), custom_call_target="tpu_custom_call" | custom-call | tf_op jit(solution)/shard_map/owner_last/pallas_call | solution.py:572
  102.5 2.6 %all-to-all-start.5 = ((f32[32,1,1280]{2,1,0:T(1,128)}), f32[32,1,1280]{2,1,0:T(1,128)S(1)}, u32[]{:S(2)}, u32[]{:S(2)}) async-start(f32[32,1,1280]{2,1,0:T(1,128)} %bitcast.13), calls=%async_computation.5 | async-start | bytes 327680 | tf_op jit(solution)/shard_map/all_to_all | solution.py:656
  105.1 5.5 %all_gather.3.agreed = f32[192,128]{1,0:T(8,128)S(1)} all-gather(f32[48,128]{1,0:T(8,128)S(1)} %get-tuple-element.59), channel_id=1, replica_groups=mesh['sub'=8,'fdr'=4] {'fdr'}, dimensions={0}, use_global_device_ids=true | all-gather | bytes 122880 | tf_op jit(solution)/shard_map/all_gather | solution.py:709
  110.6 3.1 %all-to-all-done.5 = f32[32,1,1280]{2,1,0:T(1,128)S(1)} async-done(((f32[32,1,1280]{2,1,0:T(1,128)}), f32[32,1,1280]{2,1,0:T(1,128)S(1)}, u32[]{:S(2)}, u32[]{:S(2)}) %all-to-all-start.5) | async-done | bytes 163872 | tf_op jit(solution)/shard_map/all_to_all | solution.py:656
  113.7 1.2 %finish.1 = (f32[6,32,128]{2,1,0:T(8,128)}, f32[6,32,128]{2,1,0:T(8,128)}, f32[2,5]{1,0:T(2,128)}) custom-call(s32[32]{0:T(128)S(4)} %get-tuple-element.34.base, f32[320,128]{1,0:T(8,128)S(1)} %bitcast.22, f32[192,128]{1,0:T(8,128)S(1)} %all_gather.3.agreed), custom_call_target="tpu_custom_call" | custom-call | tf_op jit(solution)/shard_map/finish/pallas_call | solution.py:572
Async XLA Ops:
  1.3 29.9 %copy-start = (f32[32,6,128]{2,0,1:T(8,128)S(1)}, f32[32,6,128]{2,0,1:T(8,128)}, u32[]{:S(2)}) copy-start(f32[32,6,128]{2,0,1:T(8,128)} %param.17) | copy-start | bytes 294916
  1.3 29.9 %copy-start.2 = (f32[32]{0:T(128)S(1)}, f32[32]{0:T(128)}, u32[]{:S(2)}) copy-start(f32[32]{0:T(128)} %weight.1) | copy-start | bytes 388
  1.3 45.4 %copy-start.1 = (s32[32,6]{0,1:T(8,128)S(1)}, s32[32,6]{0,1:T(8,128)}, u32[]{:S(2)}) copy-start(s32[32,6]{0,1:T(8,128)} %param.13) | copy-start | bytes 2308
  11.8 19.4 %all-to-all-start = ((f32[32,1,2560]{2,1,0:T(1,128)}), f32[32,1,2560]{2,1,0:T(1,128)S(1)}, u32[]{:S(2)}, u32[]{:S(2)}) async-start(f32[32,1,2560]{2,1,0:T(1,128)} %bitcast.3), calls=%async_computation | async-start | bytes 655360 | tf_op jit(solution)/shard_map/all_to_all | solution.py:656
  102.5 11.2 %all-to-all-start.5 = ((f32[32,1,1280]{2,1,0:T(1,128)}), f32[32,1,1280]{2,1,0:T(1,128)S(1)}, u32[]{:S(2)}, u32[]{:S(2)}) async-start(f32[32,1,1280]{2,1,0:T(1,128)} %bitcast.13), calls=%async_computation.5 | async-start | bytes 327680 | tf_op jit(solution)/shard_map/all_to_all | solution.py:656

commit v4 on v3

--- a/solution.py
+++ b/solution.py
@@ -111,24 +111,21 @@
 
 
 def sweep(slots, body):
-    body(0, PIECE)
-    body(PIECE, PIECE)
-
     def step(i, carry):
-        body((i + 1) * GROUP, GROUP)
+        body(i * GROUP, GROUP)
         return carry
 
-    lax.fori_loop(0, slots // GROUP - 1, step, 0)
+    lax.fori_loop(0, slots // GROUP, step, 0)
 
 
 def pick(work, iface, f, q):
     return work[pl.ds(iface[q, f], 1), :]
 
 
-def feeder_first(geo, iface, sub, live, inverse, cost, lower, upper,
-                 rounded, kept, lim, base, send,
+def feeder_first(geo, rows_in, sub_in, live, slice_index, inverse, cost, lower, upper,
+                 rounded, kept, lim, base, iface, send,
                  inv, price, out, sems, out_sems,
-                 stage1, stage2, meta, count, rank, edge, edge_sems, turned, *works):
+                 stage1, stage2, meta, count, rank, sub, edge, edge_sems, turned, *works):
     F, K, Q, NB, X = geo.F, geo.K, geo.Q, geo.NB, geo.X
     chunk = 2 * X + 2
     bound, square, left, ahead = (works[i * GROUP : (i + 1) * GROUP] for i in range(4))
@@ -138,11 +135,17 @@
         pltpu.make_async_copy(x, edge.at[pl.ds(i * F, F)], edge_sems.at[i])
         for i, x in enumerate((lower, upper))
     ]
-    for copy in sides:
+    tables = [
+        pltpu.make_async_copy(x, y, edge_sems.at[2 + i])
+        for i, (x, y) in enumerate(((sub_in, sub), (rows_in, iface)))
+    ]
+    for copy in tables + sides:
         copy.start()
     for c in range(pieces):
         for i in range(2):
             load(i, c).start()
+    for copy in tables:
+        copy.wait()
     for k in range(NB):
         count[k] = 0
 
@@ -311,7 +314,9 @@
     return qp, rp
 
 
-def owner_setup(geo, slice_index, weight, aim, recv, coef, hot_t, hot, act, scaled, den, count):
+def owner_setup(
+    geo, slice_index, weight, aim, copies, recv, coef, hot_t, hot, act, scaled, den, count
+):
     X, D, S, Q, Q2, R2, RP, PR = geo.X, geo.D, geo.S, geo.Q, geo.Q2, geo.R2, geo.RP, geo.PR
     chunk = 2 * X + 2
     metas = [recv[pl.ds(2 * X + m, D, stride=chunk), :] for m in range(2)]
@@ -337,21 +342,6 @@
             total = total + theirs
             hot_t[r2, p * S : (p + 1) * S, :] = theirs.astype(bf16)
         act[r2 * D : (r2 + 1) * D, :] = live
-    members = jnp.sum(total, axis=1, keepdims=True)
-    w = jnp.zeros((S, LANES), f32)
-    for s in range(S):
-        w = jnp.where(iota((S, LANES), 0) == s, weight[s], w)
-    members = jnp.broadcast_to(members, (S, LANES))
-    den[...] = members + w
-    qps, rps = slice_parity(geo, (S, LANES))
-    count[...] = jnp.where(rps == 0, members, 0.0)
-    lane = iota((S, LANES), 1)
-    inner = lane - (qps * RP + rps) * geo.L
-    index = inner + slice_index * geo.L
-    for q2 in range(Q2):
-        even = jnp.take_along_axis(aim[2 * q2], index, axis=1)
-        odd = jnp.take_along_axis(aim[2 * q2 + 1], index, axis=1)
-        scaled[:, q2 * LANES : (q2 + 1) * LANES] = w * jnp.where(qps == 0, even, odd)
     for par in range(2):
         for q2 in range(Q2):
             for q2p in range(Q2):
@@ -371,6 +361,23 @@
                             jnp.take_along_axis(metas[sides[1][0]], idx, axis=1),
                         )
                     coef[(par * Q2 + q2) * Q2 + q2p, r2 * D : (r2 + 1) * D, :] = value
+    for copy in copies:
+        copy.wait()
+    members = jnp.sum(total, axis=1, keepdims=True)
+    w = jnp.zeros((S, LANES), f32)
+    for s in range(S):
+        w = jnp.where(iota((S, LANES), 0) == s, weight[s], w)
+    members = jnp.broadcast_to(members, (S, LANES))
+    den[...] = members + w
+    qps, rps = slice_parity(geo, (S, LANES))
+    count[...] = jnp.where(rps == 0, members, 0.0)
+    lane = iota((S, LANES), 1)
+    inner = lane - (qps * RP + rps) * geo.L
+    index = inner + slice_index * geo.L
+    for q2 in range(Q2):
+        even = jnp.take_along_axis(aim[2 * q2], index, axis=1)
+        odd = jnp.take_along_axis(aim[2 * q2 + 1], index, axis=1)
+        scaled[:, q2 * LANES : (q2 + 1) * LANES] = w * jnp.where(qps == 0, even, odd)
 
 
 def arrive(geo, recv, chunk, off):
@@ -462,10 +469,17 @@
         ref[:, q2 * LANES : (q2 + 1) * LANES] = values[q2]
 
 
-def owner_first(geo, slice_index, weight, aim, recv,
-                send, coef, hot_t, hot, act, scaled, den, count, dual, old, norms):
+def owner_first(geo, slice_index, weight_in, aim_in, recv,
+                send, coef, hot_t, hot, act, scaled, den, count, dual, old, norms,
+                weight, aim, sems):
     X = geo.X
-    owner_setup(geo, slice_index[0], weight, aim, recv, coef, hot_t, hot, act, scaled, den, count)
+    copies = [pltpu.make_async_copy(x, y, sems.at[i])
+              for i, (x, y) in enumerate(((weight_in, weight), (aim_in, aim)))]
+    for copy in copies:
+        copy.start()
+    owner_setup(
+        geo, slice_index[0], weight, aim, copies, recv, coef, hot_t, hot, act, scaled, den, count
+    )
     tables = (coef, hot_t, hot, act, scaled, den, count)
     chunk = 2 * X + 2
     h = arrive(geo, recv, chunk, 0)
@@ -560,15 +574,12 @@
 VM = pltpu.VMEM
 SM = pltpu.SMEM
 HB = pltpu.HBM
-SMH = 0
 
 
 def call(body, args, ins, outs, scratch=(), name=None):
     args = [
-        pltpu.with_memory_space_constraint(x, HB) if s in (HB, SMH) else x
-        for x, s in zip(args, ins)
+        pltpu.with_memory_space_constraint(x, HB) if s is HB else x for x, s in zip(args, ins)
     ]
-    ins = [SM if s is SMH else s for s in ins]
     return pl.pallas_call(
         body,
         in_specs=[pl.BlockSpec(memory_space=s) for s in ins],
@@ -583,7 +594,9 @@
     )(*args)
 
 
-def feeder_calls(geo, iface, substation_of, live_count, inverse, cost, lower, upper):
+def feeder_calls(
+    geo, iface, substation_of, live_count, slice_index, inverse, cost, lower, upper
+):
     F, K, C, D, X = geo.F, geo.K, geo.C, geo.D, geo.X
     pieces = F // PIECE
     stage = pltpu.VMEM((geo.stage_rows, LANES), f32)
@@ -597,29 +610,30 @@
         return pltpu.SemaphoreType.DMA((count, pieces))
 
     def begin():
-        rounded, kept, lim, base, send = call(
+        rounded, kept, lim, base, table, send = call(
             functools.partial(feeder_first, geo),
-            (iface, substation_of, live_count, inverse, cost, lower, upper),
-            (SMH, SMH, SM, HB, HB, HB, HB),
+            (iface, substation_of, live_count, slice_index, inverse, cost, lower, upper),
+            (HB, HB, SM, SM, HB, HB, HB, HB),
             carried
             + (
                 ((K, LANES), f32, VM),
                 ((F,), i32, SM),
+                (iface.shape, i32, SM),
                 ((D * (2 * X + 2), LANES), f32, VM),
             ),
             (squares, prices, halves, sems(2), sems(1),
              stage, stage, pltpu.VMEM((2 * geo.NB, LANES), f32), pltpu.SMEM((geo.NB,), i32),
-             pltpu.SMEM((F,), i32), pltpu.VMEM((LANES, K), f32),
-             pltpu.SemaphoreType.DMA((2,)), pltpu.VMEM((K, LANES), f32)) + works,
+             pltpu.SMEM((F,), i32), pltpu.SMEM((F,), i32), pltpu.VMEM((LANES, K), f32),
+             pltpu.SemaphoreType.DMA((4,)), pltpu.VMEM((K, LANES), f32)) + works,
             "feeder_first",
         )
-        return (rounded, kept, lim, base), base, send
+        return (rounded, kept, lim, base, table), base, send
 
     def advance(state, recv, last):
-        rounded, kept, lim, base = state
+        rounded, kept, lim, base, table = state
         out = call(
             functools.partial(feeder_pair, geo, last),
-            (iface, base, live_count, inverse, cost, rounded, kept, lim, recv),
+            (table, base, live_count, inverse, cost, rounded, kept, lim, recv),
             (SM, SM, SM, HB, HB, HB, VM, VM, VM),
             ((((F, K, C), f32, HB),) if last else carried)
             + (((D * (1 if last else 2) * X, LANES), f32, VM),),
@@ -627,7 +641,7 @@
             + (stage,) * (3 if last else 4) + (pltpu.VMEM((K, LANES), f32),) + works + works[: 2 * GROUP],
             "feeder_last" if last else "feeder_pair",
         )
-        return out if last else ((out[0], out[1], lim, base), out[2])
+        return out if last else ((out[0], out[1], lim, base, table), out[2])
 
     return begin, advance
 
@@ -658,7 +672,8 @@
 
     slice_index = lax.axis_index("fdr").astype(i32).reshape(1)
     begin, advance = feeder_calls(
-        geo, iface_rows.T, substation_of, live_count, inverse, cost, lower_limit, upper_limit
+        geo, iface_rows.T, substation_of, live_count, slice_index,
+        inverse, cost, lower_limit, upper_limit,
     )
     feeders, base, send = begin()
     state = (
@@ -669,7 +684,7 @@
     out = call(
         functools.partial(owner_first, geo),
         (slice_index, reserve_weight, jnp.swapaxes(reserve_target, 0, 1), swap(send)),
-        (SM, SM, VM, VM),
+        (SM, HB, HB, VM),
         (
             ((D * 2 * X, LANES), f32, VM),
             ((2 * Q2 * Q2, n, LANES), f32, VM),
@@ -681,7 +696,7 @@
             ((S, LANES), f32, VM),
         )
         + state,
-        (),
+        (pltpu.SMEM((S,), f32), pltpu.VMEM((Q, S, C), f32), pltpu.SemaphoreType.DMA((2,))),
         "owner_first",
     )
     send, tables, memory = out[0], out[1:8], out[8:]

time: 115 us -> 112 us (0.974)
  blocking collectives: 56.5 us -> 75.7 us
  waiting for transfers between devices: 15.1 us -> 3.08 us
  starting transfers between devices: 9.89 us -> 2.58 us
  Pallas kernels: 32 us -> 28.8 us
    all_to_all x4 -> x5, blocking collectives: 51 us -> 70.1 us  [swap(): lax.all_to_all(y, ('sub', 'fdr'), split_axis=0, concat_axis=0, tiled=True)]
    all_to_all x2 -> x1, waiting for transfers between devices: 15.1 us -> 3.08 us  [swap(): lax.all_to_all(y, ('sub', 'fdr'), split_axis=0, concat_axis=0, tiled=True)]
    all_to_all x2 -> x1, starting transfers between devices: 9.89 us -> 2.58 us  [swap(): lax.all_to_all(y, ('sub', 'fdr'), split_axis=0, concat_axis=0, tiled=True)]
    pallas_call x7, Pallas kernels: 32 us -> 28.8 us  [call(): pl.pallas_call(body, in_specs=[pl.BlockSpec(memory_space=s) for s in ins]...]
  transfers between devices with their start and end apart: 2 -> 1, of which waited for: 2 -> 1; matrix products, arithmetic and copies ran while one was open for 0% -> 0% of each run, Pallas kernels for 0% -> 0%
where the time goes in v4:
time: 112 us; the launch traced here: 111 us
  blocking collectives  75.7 us (68%)
  Pallas kernels  28.8 us (26%)
  waiting for transfers between devices  3.08 us (3%)
  starting transfers between devices  2.58 us (2%)
  between operations  1.33 us (1%)
    all_to_all x5, blocking collectives, swap(): lax.all_to_all(y, ('sub', 'fdr'), split_axis=0, concat_axis=0, tiled=True)  70.1 us
    pallas_call x7, Pallas kernels, call(): pl.pallas_call(body, in_specs=[pl.BlockSpec(memory_space=s) for s in ins]...  28.8 us
    all_gather x1, blocking collectives, shards(): gathered = lax.all_gather(agreed, 'fdr', axis=0, tiled=True)  5.55 us
    all_to_all x1, waiting for transfers between devices, swap(): lax.all_to_all(y, ('sub', 'fdr'), split_axis=0, concat_axis=0, tiled=True)  3.08 us
    all_to_all x1, starting transfers between devices, swap(): lax.all_to_all(y, ('sub', 'fdr'), split_axis=0, concat_axis=0, tiled=True)  2.58 us
  transfers between devices with their start and end apart: 1, of which 1 were waited for; matrix products, arithmetic and copies ran while one was open for 0% of the time, Pallas kernels for 0%

profile of v4, /device:TPU:0, one launch (start us, length us, event | category | flops | bytes accessed | tf_op | source)
XLA Modules:
  0.0 111.5 jit_solution(8558756317643292932)
XLA Ops:
  1.3 8.5 %feeder_first.1 = (bf16[32,256,128]{2,1,0:T(8,128)(2,1)}, f32[32,8,128]{2,1,0:T(8,128)S(1)}, f32[256,128]{1,0:T(8,128)S(1)}, s32[32]{0:T(128)S(4)}, s32[6,32]{1,0:T(8,128)S(4)}, /*index=5*/f32[640,128]{1,0:T(8,128)S(1)}) custom-call(s32[6,32]{1,0:T(8,128)} %bitcast.30, s32[32]{0:T(128)} %sub_in.1, s32[1]{0:T(128)S(6)} %copy.19.live, s32[1]{0:T(128)} %bitcast.1.slice_index, ...), custom_call_target="tpu_custom_call" | custom-call | tf_op jit(solution)/shard_map/feeder_first/pallas_call | solution.py:583
  9.8 19.2 %all_to_all.30 = f32[32,1,2560]{2,1,0:T(1,128)S(1)} all-to-all(f32[32,1,2560]{2,1,0:T(1,128)S(1)} %bitcast.24), channel_id=1, replica_groups=mesh['sub'=8,'fdr'=4] {'sub','fdr'}, dimensions={0} | all-to-all | bytes 655360 | tf_op jit(solution)/shard_map/all_to_all | solution.py:670
  29.0 2.1 %owner_first.1 = (f32[576,128]{1,0:T(8,128)S(1)}, f32[18,96,128]{2,1,0:T(8,128)S(1)}, bf16[3,64,32]{2,1,0:T(8,128)(2,1)S(1)}, bf16[192,32]{1,0:T(8,128)(2,1)S(1)...) custom-call(s32[1]{0:T(128)} %bitcast.1.slice_index, ...), custom_call_target="tpu_custom_call" | custom-call | tf_op jit(solution)/shard_map/owner_first/pallas_call | solution.py:583
  31.1 13.5 %all_to_all.31 = f32[32,1,2304]{2,1,0:T(1,128)S(1)} all-to-all(f32[32,1,2304]{2,1,0:T(1,128)S(1)} %bitcast.25), channel_id=1, replica_groups=mesh['sub'=8,'fdr'=4] {'sub','fdr'}, dimensions={0} | all-to-all | bytes 589824 | tf_op jit(solution)/shard_map/all_to_all | solution.py:670
  44.6 7.6 %feeder_pair.1 = (bf16[32,256,128]{2,1,0:T(8,128)(2,1)}, f32[32,8,128]{2,1,0:T(8,128)S(1)}, f32[576,128]{1,0:T(8,128)S(1)}) custom-call(s32[6,32]{1,0:T(8,128)S(4)} %get-tuple-element.36.iface, s32[32]{0:T(128)S(4)} %get-tuple-element.35.base, s32[1]{0:T(128)S(6)} %copy.19.live, bf16[32,256,256]{2,1,0:T(8,128)(2,1)} %inverse.5, f32[32,256,128]{2,1,0:T(8,128)} %cost.5, ...), custom_call_target="tpu_custom_call" | custom-call | tf_op jit(solution)/shard_map/feeder_pair/pallas_call | solution.py:583
  52.3 13.5 %all_to_all.32 = f32[32,1,2304]{2,1,0:T(1,128)S(1)} all-to-all(f32[32,1,2304]{2,1,0:T(1,128)S(1)} %bitcast.27), channel_id=1, replica_groups=mesh['sub'=8,'fdr'=4] {'sub','fdr'}, dimensions={0} | all-to-all | bytes 589824 | tf_op jit(solution)/shard_map/all_to_all | solution.py:670
  65.7 1.2 %owner_middle.1 = (f32[576,128]{1,0:T(8,128)S(1)}, f32[96,384]{1,0:T(8,128)S(1)}, f32[32,384]{1,0:T(8,128)S(1)}, f32[16,128]{1,0:T(8,128)S(1)}) custom-call(f32[576,128]{1,0:T(8,128)S(1)} %bitcast.19, f32[18,96,128]{2,1,0:T(8,128)S(1)} %get-tuple-element.45.coef, bf16[3,64,32]{2,1,0:T(8,128)(2,1)S(1)} %get-tuple-element.46.hot_t, ...), custom_call_target="tpu_custom_call" | custom-call | tf_op jit(solution)/shard_map/owner_middle/pallas_call | solution.py:583
  66.9 13.5 %all_to_all.33 = f32[32,1,2304]{2,1,0:T(1,128)S(1)} all-to-all(f32[32,1,2304]{2,1,0:T(1,128)S(1)} %bitcast.26), channel_id=1, replica_groups=mesh['sub'=8,'fdr'=4] {'sub','fdr'}, dimensions={0} | all-to-all | bytes 589824 | tf_op jit(solution)/shard_map/all_to_all | solution.py:670
  80.4 6.8 %feeder_last.1 = (f32[32,256,128]{2,1,0:T(8,128)}, f32[288,128]{1,0:T(8,128)S(1)}) custom-call(s32[6,32]{1,0:T(8,128)S(4)} %get-tuple-element.36.iface, s32[32]{0:T(128)S(4)} %get-tuple-element.35.base, s32[1]{0:T(128)S(6)} %copy.19.live, bf16[32,256,256]{2,1,0:T(8,128)(2,1)} %inverse.5, f32[32,256,128]{2,1,0:T(8,128)} %cost.5, ...), custom_call_target="tpu_custom_call" | custom-call | tf_op jit(solution)/shard_map/feeder_last/pallas_call | solution.py:583
  87.3 10.5 %all_to_all.34 = f32[32,1,1152]{2,1,0:T(1,128)S(1)} all-to-all(f32[32,1,1152]{2,1,0:T(1,128)S(1)} %bitcast.28), channel_id=1, replica_groups=mesh['sub'=8,'fdr'=4] {'sub','fdr'}, dimensions={0} | all-to-all | bytes 294912 | tf_op jit(solution)/shard_map/all_to_all | solution.py:670
  97.7 1.3 %owner_last.1 = (f32[320,128]{1,0:T(8,128)}, f32[48,128]{1,0:T(8,128)S(1)}) custom-call(f32[288,128]{1,0:T(8,128)S(1)} %bitcast.23, f32[18,96,128]{2,1,0:T(8,128)S(1)} %get-tuple-element.45.coef, bf16[3,64,32]{2,1,0:T(8,128)(2,1)S(1)} %get-tuple-element.46.hot_t, bf16[192,32]{1,0:T(8,128)(2,1)S(1)} %get-tuple-element.47.hot, ...), custom_call_target="tpu_custom_call" | custom-call | tf_op jit(solution)/shard_map/owner_last/pallas_call | solution.py:583
  99.1 2.6 %all-to-all-start.5 = ((f32[32,1,1280]{2,1,0:T(1,128)}), f32[32,1,1280]{2,1,0:T(1,128)S(1)}, u32[]{:S(2)}, u32[]{:S(2)}) async-start(f32[32,1,1280]{2,1,0:T(1,128)} %bitcast.13), calls=%async_computation.5 | async-start | bytes 327680 | tf_op jit(solution)/shard_map/all_to_all | solution.py:670
  101.6 5.5 %all_gather.3.agreed = f32[192,128]{1,0:T(8,128)S(1)} all-gather(f32[48,128]{1,0:T(8,128)S(1)} %get-tuple-element.61), channel_id=1, replica_groups=mesh['sub'=8,'fdr'=4] {'fdr'}, dimensions={0}, use_global_device_ids=true | all-gather | bytes 122880 | tf_op jit(solution)/shard_map/all_gather | solution.py:724
  107.2 3.1 %all-to-all-done.5 = f32[32,1,1280]{2,1,0:T(1,128)S(1)} async-done(((f32[32,1,1280]{2,1,0:T(1,128)}), f32[32,1,1280]{2,1,0:T(1,128)S(1)}, u32[]{:S(2)}, u32[]{:S(2)}) %all-to-all-start.5) | async-done | bytes 163872 | tf_op jit(solution)/shard_map/all_to_all | solution.py:670
  110.3 1.2 %finish.1 = (f32[6,32,128]{2,1,0:T(8,128)}, f32[6,32,128]{2,1,0:T(8,128)}, f32[2,5]{1,0:T(2,128)}) custom-call(s32[32]{0:T(128)S(4)} %get-tuple-element.35.base, f32[320,128]{1,0:T(8,128)S(1)} %bitcast.22, f32[192,128]{1,0:T(8,128)S(1)} %all_gather.3.agreed), custom_call_target="tpu_custom_call" | custom-call | tf_op jit(solution)/shard_map/finish/pallas_call | solution.py:583
Async XLA Ops:
  99.1 11.2 %all-to-all-start.5 = ((f32[32,1,1280]{2,1,0:T(1,128)}), f32[32,1,1280]{2,1,0:T(1,128)S(1)}, u32[]{:S(2)}, u32[]{:S(2)}) async-start(f32[32,1,1280]{2,1,0:T(1,128)} %bitcast.13), calls=%async_computation.5 | async-start | bytes 327680 | tf_op jit(solution)/shard_map/all_to_all | solution.py:670

commit v5 on v4

--- a/solution.py
+++ b/solution.py
@@ -12,7 +12,7 @@
 LANES = 128
 THIN = 16
 GROUP = 8
-PIECE = 4
+PIECE = 8
 
 f32 = jnp.float32
 bf16 = jnp.bfloat16
@@ -107,30 +107,40 @@
         part = pl.ds(c * size, size)
         return pltpu.make_async_copy(src.at[part], dst.at[part], sems.at[i, c])
 
-    return pairs[0][0].shape[0] // size, one
+    return min(pairs[0][0].shape[0], pairs[0][1].shape[0]) // size, one
 
 
 def sweep(slots, body):
-    def step(i, carry):
-        body(i * GROUP, GROUP)
-        return carry
-
-    lax.fori_loop(0, slots // GROUP, step, 0)
+    for near in (False, True):
+
+        def step(i, carry, near=near):
+            body(i * GROUP, GROUP, near)
+            return carry
+
+        half = slots // 2 // GROUP
+        lax.fori_loop(half if near else 0, 2 * half if near else half, step, 0)
 
 
 def pick(work, iface, f, q):
     return work[pl.ds(iface[q, f], 1), :]
 
 
+def put(f, t, near, out, nearby):
+    if near:
+        nearby[f - nearby.shape[0]] = t
+    else:
+        out[f] = t
+
+
 def feeder_first(geo, rows_in, sub_in, live, slice_index, inverse, cost, lower, upper,
-                 rounded, kept, lim, base, iface, send,
+                 far, nearby, kept, lim, base, iface, send,
                  inv, price, out, sems, out_sems,
                  stage1, stage2, meta, count, rank, sub, edge, edge_sems, turned, *works):
     F, K, Q, NB, X = geo.F, geo.K, geo.Q, geo.NB, geo.X
     chunk = 2 * X + 2
     bound, square, left, ahead = (works[i * GROUP : (i + 1) * GROUP] for i in range(4))
     pieces, load = moves(((inverse, inv), (cost, price)), sems, PIECE)
-    _, store = moves(((out, rounded),), out_sems, PIECE)
+    far_pieces, store = moves(((out, far),), out_sems, PIECE)
     sides = [
         pltpu.make_async_copy(x, edge.at[pl.ds(i * F, F)], edge_sems.at[i])
         for i, x in enumerate((lower, upper))
@@ -172,17 +182,17 @@
         third = third + jnp.where(lane >= i * geo.PR * Q, 1, 0)
     within = lane - third * (geo.PR * Q)
 
-    def body(at, size):
+    def body(at, size, near):
         for c in range(size // PIECE):
             for i in range(2):
                 load(i, at // PIECE + c).wait()
         fs = [at + u for u in range(size)]
         turned[...] = pltpu.roll(lim[...], LANES - at, 1)
         for u, f in enumerate(fs):
-            near = within - rank[f] * Q
+            place_of = within - rank[f] * Q
             chosen = jnp.full((1, LANES), -1, i32)
             for q in range(Q):
-                chosen = jnp.where((near == q) & (third < geo.Q2), iface[q, f], chosen)
+                chosen = jnp.where((place_of == q) & (third < geo.Q2), iface[q, f], chosen)
             hot = (iota((K, LANES), 0) == jnp.broadcast_to(chosen, (K, LANES))).astype(f32)
             price_u = price[f]
             both = dot(inv[f], jnp.concatenate([-price_u, hot], axis=1).astype(bf16))
@@ -193,9 +203,9 @@
             t = clip(primal, low, high) - price_u
             left[u][...] = t
             t = t.astype(bf16)
-            out[f] = t
+            put(f, t, near, out, nearby)
             ahead[u][...] = dot(inv[f], t)
-            if u % PIECE == PIECE - 1:
+            if not near and u % PIECE == PIECE - 1:
                 store(0, at // PIECE + u // PIECE).start()
         for u, f in enumerate(fs):
             k = lax.div(sub[f], geo.S)
@@ -221,7 +231,7 @@
             send[pl.ds(j * chunk + 2 * X + m, NB, stride=geo.G * chunk), :] = meta[
                 m * NB : (m + 1) * NB
             ]
-    for c in range(pieces):
+    for c in range(far_pieces):
         store(0, c).wait()
 
 
@@ -232,21 +242,21 @@
         work[pl.ds(iface[q, f], 1), :] = rows[q]
 
 
-def feeder_pair(geo, last, iface, base, live, inverse, cost, rounded, kept, lim, recv, *rest):
+def feeder_pair(geo, last, iface, base, live, inverse, cost, far, nearby, kept, lim, recv, *rest):
     if last:
         result, send, inv, price, held, out, sems, out_sems = rest[:8]
         rest = rest[8:]
     else:
-        result, kept_out, send, inv, price, held, out, sems, out_sems = rest[:9]
-        rest = rest[9:]
+        result, nearby_out, kept_out, send, inv, price, held, out, sems, out_sems = rest[:10]
+        rest = rest[10:]
     ways = 1 if last else 2
     arrived, leaving, works = rest[:2], rest[2 : 2 + ways], rest[2 + ways :]
     turned, works = works[0], works[1:]
     side, bound, left, ahead, lows, highs = (works[i * GROUP : (i + 1) * GROUP] for i in range(6))
-    pieces, load = moves(((inverse, inv), (cost, price), (rounded, held)), sems, PIECE)
-    _, store = moves(((out, result),), out_sems, PIECE)
+    pieces, load = moves(((inverse, inv), (cost, price), (far, held)), sems, PIECE)
+    out_pieces, store = moves(((out, result),), out_sems, PIECE)
     for c in range(pieces):
-        for i in range(3):
+        for i in range(3 if 2 * c < pieces else 2):
             load(i, c).start()
     for s in range(2):
         unpack(geo, recv, arrived[s], 2 * geo.X, s * geo.X)
@@ -255,14 +265,14 @@
     if not last:
         kept_out[...] = jnp.zeros_like(kept_out)
 
-    def body(at, size):
+    def body(at, size, near):
         for c in range(size // PIECE):
-            for i in range(3):
+            for i in range(2 if near else 3):
                 load(i, at // PIECE + c).wait()
         fs = [at + u for u in range(size)]
         turned[...] = pltpu.roll(lim[...], LANES - at, 1)
         for u, f in enumerate(fs):
-            side[u][...] = held[f].astype(f32)
+            side[u][...] = (nearby[f - nearby.shape[0]] if near else held[f]).astype(f32)
             rows = [kept[f, q : q + 1, :] for q in range(geo.Q)]
             raise_rows(geo, f, iface, base, rows, side[u], arrived[0])
         for u, f in enumerate(fs):
@@ -284,9 +294,9 @@
                 t = anchor - price[f]
                 side[u][...] = t
                 t = t.astype(bf16)
-                out[f] = t
+                put(f, t, near, out, nearby_out)
                 ahead[u][...] = dot(inv[f], t)
-            if u % PIECE == PIECE - 1:
+            if (last or not near) and u % PIECE == PIECE - 1:
                 store(0, at // PIECE + u // PIECE).start()
         for u, f in enumerate(fs):
             to = base[f]
@@ -299,7 +309,7 @@
     sweep(geo.F, body)
     for s in range(ways):
         pack(geo, leaving[s], send, ways * geo.X, s * geo.X)
-    for c in range(pieces):
+    for c in range(out_pieces):
         store(0, c).wait()
 
 
@@ -603,14 +613,15 @@
     works = (pltpu.VMEM((K, LANES), f32),) * (4 * GROUP)
     squares = pltpu.VMEM((F, K, K), bf16)
     prices = pltpu.VMEM((F, K, C), f32)
-    halves = pltpu.VMEM((F, K, C), bf16)
-    carried = (((F, K, C), bf16, HB), ((F, 8, C), f32, VM))
+    halves = pltpu.VMEM((F // 2, K, C), bf16)
+    half = (F // 2, K, C)
+    carried = ((half, bf16, HB), (half, bf16, VM), ((F, 8, C), f32, VM))
 
     def sems(count):
         return pltpu.SemaphoreType.DMA((count, pieces))
 
     def begin():
-        rounded, kept, lim, base, table, send = call(
+        far, nearby, kept, lim, base, table, send = call(
             functools.partial(feeder_first, geo),
             (iface, substation_of, live_count, slice_index, inverse, cost, lower, upper),
             (HB, HB, SM, SM, HB, HB, HB, HB),
@@ -627,21 +638,21 @@
              pltpu.SemaphoreType.DMA((4,)), pltpu.VMEM((K, LANES), f32)) + works,
             "feeder_first",
         )
-        return (rounded, kept, lim, base, table), base, send
+        return (far, nearby, kept, lim, base, table), base, send
 
     def advance(state, recv, last):
-        rounded, kept, lim, base, table = state
+        far, nearby, kept, lim, base, table = state
         out = call(
             functools.partial(feeder_pair, geo, last),
-            (table, base, live_count, inverse, cost, rounded, kept, lim, recv),
-            (SM, SM, SM, HB, HB, HB, VM, VM, VM),
+            (table, base, live_count, inverse, cost, far, nearby, kept, lim, recv),
+            (SM, SM, SM, HB, HB, HB, VM, VM, VM, VM),
             ((((F, K, C), f32, HB),) if last else carried)
             + (((D * (1 if last else 2) * X, LANES), f32, VM),),
             (squares, prices, halves, prices if last else halves, sems(3), sems(1))
             + (stage,) * (3 if last else 4) + (pltpu.VMEM((K, LANES), f32),) + works + works[: 2 * GROUP],
             "feeder_last" if last else "feeder_pair",
         )
-        return out if last else ((out[0], out[1], lim, base, table), out[2])
+        return out if last else ((*out[:3], lim, base, table), out[3])
 
     return begin, advance
 

time: 112 us -> 111 us (level)
  no operation moved by 1% of the time
where the time goes in v5:
time: 111 us
  blocking collectives  75.7 us (68%)
  Pallas kernels  27.9 us (25%)
  waiting for transfers between devices  3.08 us (3%)
  starting transfers between devices  2.58 us (2%)
  between operations  1.33 us (1%)
    all_to_all x5, blocking collectives, swap(): lax.all_to_all(y, ('sub', 'fdr'), split_axis=0, concat_axis=0, tiled=True)  70.2 us
    pallas_call x7, Pallas kernels, call(): pl.pallas_call(body, in_specs=[pl.BlockSpec(memory_space=s) for s in ins]...  27.9 us
    all_gather x1, blocking collectives, shards(): gathered = lax.all_gather(agreed, 'fdr', axis=0, tiled=True)  5.55 us
    all_to_all x1, waiting for transfers between devices, swap(): lax.all_to_all(y, ('sub', 'fdr'), split_axis=0, concat_axis=0, tiled=True)  3.08 us
    all_to_all x1, starting transfers between devices, swap(): lax.all_to_all(y, ('sub', 'fdr'), split_axis=0, concat_axis=0, tiled=True)  2.58 us
  transfers between devices with their start and end apart: 1, of which 1 were waited for; matrix products, arithmetic and copies ran while one was open for 0% of the time, Pallas kernels for 0%

profile of v5, /device:TPU:0, one launch (start us, length us, event | category | flops | bytes accessed | tf_op | source)
XLA Modules:
  0.0 110.6 jit_solution(16540712176668519227)
XLA Ops:
  1.3 7.9 %feeder_first.1 = (bf16[16,256,128]{2,1,0:T(8,128)(2,1)}, bf16[16,256,128]{2,1,0:T(8,128)(2,1)S(1)}, f32[32,8,128]{2,1,0:T(8,128)S(1)}, f32[256,128]{1,0:T(8,128...) custom-call(s32[6,32]{1,0:T(8,128)} %bitcast.30, s32[32]{0:T(128)} %sub_in.1, s32[1]{0:T(128)S(6)} %copy.19.live, ...), custom_call_target="tpu_custom_call" | custom-call | tf_op jit(solution)/shard_map/feeder_first/pallas_call | solution.py:593
  9.2 19.2 %all_to_all.30 = f32[32,1,2560]{2,1,0:T(1,128)S(1)} all-to-all(f32[32,1,2560]{2,1,0:T(1,128)S(1)} %bitcast.24), channel_id=1, replica_groups=mesh['sub'=8,'fdr'=4] {'sub','fdr'}, dimensions={0} | all-to-all | bytes 655360 | tf_op jit(solution)/shard_map/all_to_all | solution.py:681
  28.4 2.1 %owner_first.1 = (f32[576,128]{1,0:T(8,128)S(1)}, f32[18,96,128]{2,1,0:T(8,128)S(1)}, bf16[3,64,32]{2,1,0:T(8,128)(2,1)S(1)}, bf16[192,32]{1,0:T(8,128)(2,1)S(1)...) custom-call(s32[1]{0:T(128)} %bitcast.1.slice_index, ...), custom_call_target="tpu_custom_call" | custom-call | tf_op jit(solution)/shard_map/owner_first/pallas_call | solution.py:593
  30.5 13.5 %all_to_all.31 = f32[32,1,2304]{2,1,0:T(1,128)S(1)} all-to-all(f32[32,1,2304]{2,1,0:T(1,128)S(1)} %bitcast.25), channel_id=1, replica_groups=mesh['sub'=8,'fdr'=4] {'sub','fdr'}, dimensions={0} | all-to-all | bytes 589824 | tf_op jit(solution)/shard_map/all_to_all | solution.py:681
  44.1 7.2 %feeder_pair.1 = (bf16[16,256,128]{2,1,0:T(8,128)(2,1)}, bf16[16,256,128]{2,1,0:T(8,128)(2,1)S(1)}, f32[32,8,128]{2,1,0:T(8,128)S(1)}, f32[576,128]{1,0:T(8,128)S(1)}) custom-call(s32[6,32]{1,0:T(8,128)S(4)} %get-tuple-element.38.iface, s32[32]{0:T(128)S(4)} %get-tuple-element.37.base, s32[1]{0:T(128)S(6)} %copy.19.live, bf16[32,256,256]{2,1,0:T(8,128)(2,1)} %inverse.5, ...), custom_call_target="tpu_custom_call" | custom-call | tf_op jit(solution)/shard_map/feeder_pair/pallas_call | solution.py:593
  51.3 13.5 %all_to_all.32 = f32[32,1,2304]{2,1,0:T(1,128)S(1)} all-to-all(f32[32,1,2304]{2,1,0:T(1,128)S(1)} %bitcast.26), channel_id=1, replica_groups=mesh['sub'=8,'fdr'=4] {'sub','fdr'}, dimensions={0} | all-to-all | bytes 589824 | tf_op jit(solution)/shard_map/all_to_all | solution.py:681
  64.8 1.2 %owner_middle.1 = (f32[576,128]{1,0:T(8,128)S(1)}, f32[96,384]{1,0:T(8,128)S(1)}, f32[32,384]{1,0:T(8,128)S(1)}, f32[16,128]{1,0:T(8,128)S(1)}) custom-call(f32[576,128]{1,0:T(8,128)S(1)} %bitcast.19, f32[18,96,128]{2,1,0:T(8,128)S(1)} %get-tuple-element.49.coef, bf16[3,64,32]{2,1,0:T(8,128)(2,1)S(1)} %get-tuple-element.50.hot_t, ...), custom_call_target="tpu_custom_call" | custom-call | tf_op jit(solution)/shard_map/owner_middle/pallas_call | solution.py:593
  66.0 13.5 %all_to_all.33 = f32[32,1,2304]{2,1,0:T(1,128)S(1)} all-to-all(f32[32,1,2304]{2,1,0:T(1,128)S(1)} %bitcast.27), channel_id=1, replica_groups=mesh['sub'=8,'fdr'=4] {'sub','fdr'}, dimensions={0} | all-to-all | bytes 589824 | tf_op jit(solution)/shard_map/all_to_all | solution.py:681
  79.5 7.0 %feeder_last.1 = (f32[32,256,128]{2,1,0:T(8,128)}, f32[288,128]{1,0:T(8,128)S(1)}) custom-call(s32[6,32]{1,0:T(8,128)S(4)} %get-tuple-element.38.iface, s32[32]{0:T(128)S(4)} %get-tuple-element.37.base, s32[1]{0:T(128)S(6)} %copy.19.live, bf16[32,256,256]{2,1,0:T(8,128)(2,1)} %inverse.5, f32[32,256,128]{2,1,0:T(8,128)} %cost.5, ...), custom_call_target="tpu_custom_call" | custom-call | tf_op jit(solution)/shard_map/feeder_last/pallas_call | solution.py:593
  86.4 10.5 %all_to_all.34 = f32[32,1,1152]{2,1,0:T(1,128)S(1)} all-to-all(f32[32,1,1152]{2,1,0:T(1,128)S(1)} %bitcast.28), channel_id=1, replica_groups=mesh['sub'=8,'fdr'=4] {'sub','fdr'}, dimensions={0} | all-to-all | bytes 294912 | tf_op jit(solution)/shard_map/all_to_all | solution.py:681
  96.9 1.3 %owner_last.1 = (f32[320,128]{1,0:T(8,128)}, f32[48,128]{1,0:T(8,128)S(1)}) custom-call(f32[288,128]{1,0:T(8,128)S(1)} %bitcast.23, f32[18,96,128]{2,1,0:T(8,128)S(1)} %get-tuple-element.49.coef, bf16[3,64,32]{2,1,0:T(8,128)(2,1)S(1)} %get-tuple-element.50.hot_t, bf16[192,32]{1,0:T(8,128)(2,1)S(1)} %get-tuple-element.51.hot, ...), custom_call_target="tpu_custom_call" | custom-call | tf_op jit(solution)/shard_map/owner_last/pallas_call | solution.py:593
  98.2 2.6 %all-to-all-start.5 = ((f32[32,1,1280]{2,1,0:T(1,128)}), f32[32,1,1280]{2,1,0:T(1,128)S(1)}, u32[]{:S(2)}, u32[]{:S(2)}) async-start(f32[32,1,1280]{2,1,0:T(1,128)} %bitcast.13), calls=%async_computation.5 | async-start | bytes 327680 | tf_op jit(solution)/shard_map/all_to_all | solution.py:681
  100.8 5.5 %all_gather.3.agreed = f32[192,128]{1,0:T(8,128)S(1)} all-gather(f32[48,128]{1,0:T(8,128)S(1)} %get-tuple-element.65), channel_id=1, replica_groups=mesh['sub'=8,'fdr'=4] {'fdr'}, dimensions={0}, use_global_device_ids=true | all-gather | bytes 122880 | tf_op jit(solution)/shard_map/all_gather | solution.py:735
  106.4 3.1 %all-to-all-done.5 = f32[32,1,1280]{2,1,0:T(1,128)S(1)} async-done(((f32[32,1,1280]{2,1,0:T(1,128)}), f32[32,1,1280]{2,1,0:T(1,128)S(1)}, u32[]{:S(2)}, u32[]{:S(2)}) %all-to-all-start.5) | async-done | bytes 163872 | tf_op jit(solution)/shard_map/all_to_all | solution.py:681
  109.4 1.2 %finish.1 = (f32[6,32,128]{2,1,0:T(8,128)}, f32[6,32,128]{2,1,0:T(8,128)}, f32[2,5]{1,0:T(2,128)}) custom-call(s32[32]{0:T(128)S(4)} %get-tuple-element.37.base, f32[320,128]{1,0:T(8,128)S(1)} %bitcast.22, f32[192,128]{1,0:T(8,128)S(1)} %all_gather.3.agreed), custom_call_target="tpu_custom_call" | custom-call | tf_op jit(solution)/shard_map/finish/pallas_call | solution.py:593
Async XLA Ops:
  98.2 11.2 %all-to-all-start.5 = ((f32[32,1,1280]{2,1,0:T(1,128)}), f32[32,1,1280]{2,1,0:T(1,128)S(1)}, u32[]{:S(2)}, u32[]{:S(2)}) async-start(f32[32,1,1280]{2,1,0:T(1,128)} %bitcast.13), calls=%async_computation.5 | async-start | bytes 327680 | tf_op jit(solution)/shard_map/all_to_all | solution.py:681
